TPU v7x, 32 devices: a whole 2x2x4 slice. The times are simulated.
32 devices in a mesh: rep: 2 (over y), seq: 4 (over z), head: 4 (over x, core).
Axes of the slice: x: 2, y: 2, z: 4, core: 2. Of those that a mesh axis runs over, the one named last changes fastest.
Arguments:
- queries: bfloat16 [2048, 4096], P(('rep', 'seq'), 'head'), parts along dimension 0, may hold values from -520 to 520
- rotated_key_states: bfloat16 [2048, 1024], P(('rep', 'seq'), 'head'), parts along dimension 0, may hold values from -6 to 6
- value_state_array: bfloat16 [2048, 1024], P(('rep', 'seq'), 'head'), parts along dimension 0, may hold values from -6 to 6
- residual: bfloat16 [2048, 4096], P(('rep', 'seq'), 'head'), parts along dimension 0, may hold values from -60 to 60
- out_weight: bfloat16 [4096, 4096], P('head'), may hold values from -0.75 to 0.75
- norm_gain: bfloat16 [4096], P('head'), may hold values from 0.5 to 1.5
- block_order: int32 [16], P('rep'), parts along dimension 0, may hold values from 0 to 7, as said below
Outputs:
- normed: bfloat16 [2048, 4096], P(('rep', 'seq'), 'head'), parts along dimension 0
There are 2 independent parts, one for each index of `rep`. A program takes and returns all parts, laid end to end along the dimension named above; an argument that names none is the same for every part. Nothing has to cross between parts.
Inputs may be any that keep to these rules, and one draw needn't show every extreme that they name: `block_order`: slots 2i and 2i + 1 hold blocks c and 7 - c in either order; every block appears once.
All inputs are finite; a program needn't handle non-finite values.
Results may differ from a plain program's by a relative error of at most 0.008.
Values may be sent and summed in bfloat16 or wider, within the bound.
No kernel may reach another device: no remote copies, remote signals or barrier semaphores. Data moves between devices by JAX's collectives and lax.ppermute only.
A program may use at most 64 MiB of HBM per device.

v0:
```python
import math

import jax
import jax.numpy as jnp
from jax import lax
from jax.sharding import PartitionSpec as P

D = 4096
HEAD_SIZE = 128


norm_epsilon = 1e-05


def slot_positions(row_ids, block_order, block_rows):
    slot_index = row_ids // block_rows
    slot_ids = jnp.arange(block_order.shape[0], dtype=jnp.int32)
    starts = jnp.sum(
        jnp.where(slot_index[:, None] == slot_ids[None, :], block_order[None, :], 0), axis=1
    )
    return starts * block_rows + row_ids % block_rows


def attend_block(carried, query_rows, query_positions, key_block, value_block, key_positions):
    row_peak, denominators, weighted_sum = carried
    scores = jnp.einsum(
        "qhgd,khd->hgqk", query_rows, key_block, preferred_element_type=jnp.float32
    ) * HEAD_SIZE ** (-0.5)
    visible = (key_positions[None, :] <= query_positions[:, None])[None, None]
    scores = jnp.where(visible, scores, -1e30)
    new_peak = jnp.maximum(row_peak, jnp.max(scores, axis=3))
    weights = jnp.where(visible, jnp.exp(scores - new_peak[..., None]), 0.0)
    factor = jnp.exp(row_peak - new_peak)
    denominators = denominators * factor + jnp.sum(weights, axis=3)
    weighted_sum = weighted_sum * factor[..., None] + jnp.einsum(
        "hgqk,khd->hgqd",
        weights.astype(jnp.bfloat16),
        value_block,
        preferred_element_type=jnp.float32,
    )
    return (new_peak, denominators, weighted_sum)


def body(
    queries, rotated_key_states, value_state_array, residual, out_weight, norm_gain, block_order
):
    tok_rows = queries.shape[0]
    block_rows = tok_rows // 2
    kv_heads = rotated_key_states.shape[1] // HEAD_SIZE
    heads_of_queries = queries.shape[1] // HEAD_SIZE
    queries_per_group = heads_of_queries // kv_heads
    own_rows = lax.axis_index("seq") * tok_rows + jnp.arange(tok_rows, dtype=jnp.int32)
    own_positions = slot_positions(own_rows, block_order, block_rows)
    shaped = queries.reshape(tok_rows, kv_heads, queries_per_group, HEAD_SIZE)
    query_sides = [
        (shaped[:block_rows], own_positions[:block_rows]),
        (shaped[block_rows:], own_positions[block_rows:]),
    ]

    def fresh_state():
        return (
            jnp.full((kv_heads, queries_per_group, block_rows), -1e30, jnp.float32),
            jnp.zeros((kv_heads, queries_per_group, block_rows), jnp.float32),
            jnp.zeros((kv_heads, queries_per_group, block_rows, HEAD_SIZE), jnp.float32),
        )

    key_piece = lax.all_gather(rotated_key_states, "seq", axis=0, tiled=True)
    value_piece = lax.all_gather(value_state_array, "seq", axis=0, tiled=True)
    piece_rows = key_piece.shape[0]
    width_rows = math.gcd(piece_rows, 512)
    heads_of_keys = key_piece.reshape(piece_rows, kv_heads, HEAD_SIZE)
    heads_of_values = value_piece.reshape(piece_rows, kv_heads, HEAD_SIZE)

    def one_step(block_index, states):
        offset = block_index * width_rows
        key_block = lax.dynamic_slice_in_dim(heads_of_keys, offset, width_rows, 0)
        value_block = lax.dynamic_slice_in_dim(heads_of_values, offset, width_rows, 0)
        row_ids = offset + jnp.arange(width_rows, dtype=jnp.int32)
        key_positions = slot_positions(row_ids, block_order, block_rows)
        updated = []
        for side_index in range(2):
            query_rows, query_positions = query_sides[side_index]
            updated.append(
                attend_block(
                    states[side_index],
                    query_rows,
                    query_positions,
                    key_block,
                    value_block,
                    key_positions,
                )
            )
        return tuple(updated)

    states = lax.fori_loop(0, piece_rows // width_rows, one_step, (fresh_state(), fresh_state()))
    outputs = []
    for side_state in states:
        row_peak, denominators, weighted_sum = side_state
        result = weighted_sum / denominators[..., None]
        outputs.append(
            result.transpose(2, 0, 1, 3).reshape(block_rows, heads_of_queries * HEAD_SIZE)
        )
    attention = jnp.concatenate(outputs, axis=0).astype(jnp.bfloat16)
    partial_terms = jnp.dot(attention, out_weight, preferred_element_type=jnp.float32)
    projected = lax.psum_scatter(
        partial_terms.astype(jnp.bfloat16), "head", scatter_dimension=1, tiled=True
    ).astype(jnp.float32)
    mixed_rows = residual.astype(jnp.float32) + projected
    squares = jnp.sum(mixed_rows * mixed_rows, axis=1)
    totals = lax.psum(squares, "head")
    inverse = lax.rsqrt(totals / D + norm_epsilon)
    return (mixed_rows * inverse[:, None] * norm_gain.astype(jnp.float32)[None, :]).astype(
        jnp.bfloat16
    )


def solution(mesh):
    in_specs = (
        P(("rep", "seq"), "head"),
        P(("rep", "seq"), "head"),
        P(("rep", "seq"), "head"),
        P(("rep", "seq"), "head"),
        P("head", None),
        P("head"),
        P("rep"),
    )
    out_specs = P(("rep", "seq"), "head")
    return jax.shard_map(body, mesh=mesh, in_specs=in_specs, out_specs=out_specs, check_vma=False)
```

profile of v0, /device:TPU:0, one launch (start us, length us, event | category | flops | bytes accessed | tf_op | source)
XLA Modules:
  0.0 112.1 jit_solution(11763717480250504715)
XLA Ops:
  6.5 0.0 reduce-scatter.2.cloned.1.call-start
  6.6 0.8 select_reduce_fusion.1
  7.4 1.1 fusion.48
  8.5 0.0 copy-start.8
  8.5 0.2 copy.40
  8.7 0.2 copy.29
  8.9 0.2 copy.41
  9.0 0.2 copy.31
  9.2 0.1 copy.24
  9.3 17.4 %all_gather.6 = bf16[1024,256]{0,1:T(8,128)(2,1)S(1)} all-gather(bf16[256,256]{0,1:T(8,128)(2,1)S(1)} %copy.24), channel_id=1, replica_groups=mesh['rep'=2,'seq'=4,'head'=4] {'seq'}, dimensions={0}, use_global_device_ids=true | all-gather | bytes 655360 | tf_op jit(solution)/shard_map/all_gather | solution.py:67
  26.7 0.1 copy.26
  26.8 17.1 %all_gather.7 = bf16[1024,256]{0,1:T(8,128)(2,1)} all-gather(bf16[256,256]{0,1:T(8,128)(2,1)S(1)} %copy.26), channel_id=1, replica_groups=mesh['rep'=2,'seq'=4,'head'=4] {'seq'}, dimensions={0}, use_global_device_ids=true | all-gather | bytes 655360 | tf_op jit(solution)/shard_map/all_gather | solution.py:68
  43.9 0.0 copy-done.8
  43.9 10.7 %while.26 = (s32[]{:T(128)}, f32[2,4,128]{2,1,0:T(4,128)S(1)}, f32[2,4,128]{2,1,0:T(4,128)S(1)}, f32[2,4,128,128]{3,2,1,0:T(8,128)}, f32[2,4,128]{2,1,0:T(4,128)...) while((s32[]{:T(128)}, f32[2,4,128]{2,1,0:T(4,128)S(1)}, ...), condition=%wide.region_7.8_spmd.clone, body=%wide.region_1.7_spmd.clone.sunk | while | flops 551457280 | bytes 27407780 | solution.py:95
  43.9 0.1 select_reduce_fusion.3
  44.0 0.1 broadcast_compare_fusion.4
  44.2 0.6 fusion.72
  44.8 0.5 fusion.75
  45.3 0.5 fusion.73
  45.9 0.5 fusion.74
  46.4 0.1 copy-done.4
  46.5 1.0 convolution_add_fusion.5
  47.5 0.1 copy-done.2
  47.5 1.0 convolution_add_fusion.4
  48.5 0.0 copy-start.3
  48.5 0.8 copy-done.3
  49.3 0.1 select_reduce_fusion.3
  49.4 0.1 broadcast_compare_fusion.4
  49.6 0.6 fusion.72
  50.1 0.5 fusion.75
  50.7 0.6 fusion.73
  51.3 0.5 fusion.74
  51.8 0.1 copy-done.4
  51.9 1.0 convolution_add_fusion.5
  52.9 0.1 copy-done.2
  52.9 1.0 convolution_add_fusion.4
  53.9 0.0 copy-start.3
  53.9 0.8 copy-done.3
  54.7 1.2 %copy.32 = f32[2,4,128,128]{2,3,1,0:T(8,128)S(1)} copy(f32[2,4,128,128]{3,2,1,0:T(8,128)} %get-tuple-element.341) | data formatting | bytes 1048576 | tf_op jit(solution)/shard_map/while | solution.py:95
  55.9 1.2 %copy.33 = f32[2,4,128,128]{2,3,1,0:T(8,128)S(1)} copy(f32[2,4,128,128]{3,2,1,0:T(8,128)} %get-tuple-element.343) | data formatting | bytes 1048576 | tf_op jit(solution)/shard_map/while | solution.py:95
  57.2 0.1 divide_convert_fusion
  57.3 7.1 %convolution_convert_fusion = bf16[256,4096]{1,0:T(8,128)(2,1)} fusion(bf16[1024,4096]{1,0:T(8,128)(2,1)} %param.13, bf16[128,1024]{0,1:T(8,128)(2,1)S(1)} %bitcast.84, bf16[128,1024]{0,1:T(8,128)(2,1)S(1)} %bitcast.85), kind=kOutput, calls=%fused_computation.65 | convolution fusion | flops 2149580800 | bytes 11010048 | tf_op jit(solution)/shard_map/dot_general | solution.py:104
  64.4 0.0 reduce-scatter.2.cloned.1.call-update
  64.4 0.7 copy-done.9
  65.1 31.1 %reduce-scatter.2.cloned.1.call-done = bf16[256,1024]{1,0:T(8,128)(2,1)} async-done(((bf16[256,4096]{1,0:T(8,128)(2,1)}), bf16[256,1024]{1,0:T(8,128)(2,1)}) %reduce-scatter.2.cloned.1.call-update) | async-done | bytes 524304 | tf_op jit(solution)/shard_map/reduce_scatter | solution.py:105
  96.2 1.3 %multiply_reduce_fusion = f32[256]{0:T(256)S(1)} fusion(bf16[256,1024]{1,0:T(8,128)(2,1)} %reduce-scatter.2.cloned.1.call-done, bf16[256,1024]{1,0:T(8,128)(2,1)S(1)} %copy-done), kind=kLoop, calls=%fused_computation.67 | loop fusion | flops 1310464 | bytes 1049600 | tf_op jit(solution)/shard_map/reduce_sum | solution.py:109
  97.5 5.8 %psum.7 = f32[256]{0:T(256)S(1)} all-reduce(f32[256]{0:T(256)S(1)} %multiply_reduce_fusion), channel_id=1, replica_groups=mesh['rep'=2,'seq'=4,'head'=4] {'head'}, use_global_device_ids=true, to_apply=%region_10.11 | all-reduce | flops 256 | bytes 2048 | tf_op jit(solution)/shard_map/psum | solution.py:110
  103.3 2.0 %multiply_convert_fusion = bf16[256,1024]{1,0:T(8,128)(2,1)} fusion(bf16[256,1024]{1,0:T(8,128)(2,1)} %reduce-scatter.2.cloned.1.call-done, bf16[256,1024]{1,0:T(8,128)(2,1)S(1)} %copy-done, f32[1024]{0:T(1024)S(1)} %convert_element_type.39, f32[256]{0:T(256)S(1)} %add_rsqrt_fusion), kind=kLoop, calls=%fused_computation.66 | loop fusion | flops 1572864 | bytes 1577984 | tf_op jit(solution)/shard_map/convert_element_type | solution.py:112
  (44 shorter events, 0.2 us)
Async XLA Ops:
  6.5 2.7 %copy-start.6 = (bf16[256,256]{1,0:T(8,128)(2,1)S(1)}, bf16[256,256]{1,0:T(8,128)(2,1)}, u32[]{:S(2)}) copy-start(bf16[256,256]{1,0:T(8,128)(2,1)} %param.10) | copy-start | bytes 393220
  6.5 20.2 %copy-start.7 = (bf16[256,256]{1,0:T(8,128)(2,1)S(1)}, bf16[256,256]{1,0:T(8,128)(2,1)}, u32[]{:S(2)}) copy-start(bf16[256,256]{1,0:T(8,128)(2,1)} %param.11) | copy-start | bytes 393220
  6.5 89.7 %reduce-scatter.2.cloned.1.call-start = ((), (), s32[]{:S(2)}) async-start(), calls=%async_computation.1 | async-start | bytes 2621440 | tf_op jit(solution)/shard_map/reduce_scatter | solution.py:105
  8.5 35.4 %copy-start.8 = (s32[8]{0:T(128)S(1)}, s32[8]{0:T(128)}, u32[]{:S(2)}) copy-start(s32[8]{0:T(128)} %param.15) | copy-start | bytes 100
  45.3 1.1 %copy-start.1 = (bf16[1024,2,128]{0,2,1:T(8,128)(2,1)S(1)}, bf16[1024,2,128]{0,2,1:T(8,128)(2,1)}, u32[]{:S(2)}) copy-start(bf16[1024,2,128]{0,2,1:T(8,128)(2,1)} %get-tuple-element.616) | copy-start | bytes 1572868 | tf_op jit(solution)/shard_map/while
  45.3 1.2 %copy-start.4 = (f32[2,4,128,128]{3,2,1,0:T(8,128)S(1)}, f32[2,4,128,128]{3,2,1,0:T(8,128)}, u32[]{:S(2)}) copy-start(f32[2,4,128,128]{3,2,1,0:T(8,128)} %get-tuple-element.593) | copy-start | bytes 1572868 | tf_op jit(solution)/shard_map/while
  46.5 1.0 copy-start.2
  47.5 1.0 copy-start.5
  48.5 0.8 copy-start.3
  50.7 1.1 %copy-start.1 = (bf16[1024,2,128]{0,2,1:T(8,128)(2,1)S(1)}, bf16[1024,2,128]{0,2,1:T(8,128)(2,1)}, u32[]{:S(2)}) copy-start(bf16[1024,2,128]{0,2,1:T(8,128)(2,1)} %get-tuple-element.616) | copy-start | bytes 1572868 | tf_op jit(solution)/shard_map/while
  50.7 1.2 %copy-start.4 = (f32[2,4,128,128]{3,2,1,0:T(8,128)S(1)}, f32[2,4,128,128]{3,2,1,0:T(8,128)}, u32[]{:S(2)}) copy-start(f32[2,4,128,128]{3,2,1,0:T(8,128)} %get-tuple-element.593) | copy-start | bytes 1572868 | tf_op jit(solution)/shard_map/while
  51.9 1.0 copy-start.2
  52.8 1.0 copy-start.5
  53.9 0.8 copy-start.3
  64.4 0.7 copy-start.9
  64.4 31.8 %copy-start = (bf16[256,1024]{1,0:T(8,128)(2,1)S(1)}, bf16[256,1024]{1,0:T(8,128)(2,1)}, u32[]{:S(2)}) copy-start(bf16[256,1024]{1,0:T(8,128)(2,1)} %param.12) | copy-start | bytes 1572868
Sparse Core Ops, SparseCore 0:
  64.6 31.5 reduce-scatter.1
where the time goes:
time: 113 us; the launch traced here: 112 us
  blocking collectives  40.2 us (36%)
  waiting for transfers between devices  31.1 us (28%)
  between operations  13.5 us (12%)
  matrix products  13.2 us (12%)
  other arithmetic  6.97 us (6%)
  local copies, waits for them, and re-layouts  6.94 us (6%)
    reduce_scatter x1, waiting for transfers between devices, body(): lax.psum_scatter(partial_terms.astype(jnp.bfloat16), 'head', scatter_dime...  31.1 us
    all_gather x1, blocking collectives, body(): key_piece = lax.all_gather(rotated_key_states, 'seq', axis=0, tiled=True)  17.4 us
    all_gather x1, blocking collectives, body(): value_piece = lax.all_gather(value_state_array, 'seq', axis=0, tiled=True)  17.1 us
    dot_general x1, matrix products, body(): jnp.dot(attention, out_weight, preferred_element_type=jnp.float32)  7.11 us
    psum x1, blocking collectives, body(): totals = lax.psum(squares, 'head')  5.76 us
    dot_general x4, matrix products, attend_block(): jnp.einsum('hgqk,khd->hgqd', weights.astype(jnp.bfloat16), value_block, p...  3.84 us
    while x2, local copies, waits for them, and re-layouts, body(): lax.fori_loop(0, piece_rows // width_rows, one_step, (fresh_state(), fres...  2.47 us
  transfers between devices with their start and end apart: 1, of which 1 were waited for; matrix products, arithmetic and copies ran while one was open for 0% of the time, Pallas kernels for 0%

commit v1 on v0

v1 whole, which is shorter than its diff:
```python
import functools
import math

import jax
import jax.numpy as jnp
from jax import lax
from jax.experimental import pallas as pl
from jax.experimental.pallas import tpu as pltpu
from jax.sharding import PartitionSpec as P

HEAD_SIZE = 128
norm_epsilon = 1e-05
FAR = -1e30
VMEM = pltpu.VMEM
SMEM = pltpu.SMEM
LIMIT = 40 * 2**20


def vmem_out(shape, dtype):
    return pltpu.VMEM(shape, dtype)


def whole(space):
    return pl.BlockSpec(memory_space=space)


def params():
    return pltpu.CompilerParams(vmem_limit_bytes=LIMIT)


def cost(flops, size, exps=0):
    return pl.CostEstimate(flops=flops, bytes_accessed=size, transcendentals=exps)


def early_of(order_ref, slot):
    return jnp.minimum(order_ref[2 * slot], order_ref[2 * slot + 1])


def flip_of(order_ref):
    me = lax.axis_index("seq")
    return (order_ref[2 * me] > order_ref[2 * me + 1]).astype(jnp.int32)


def half(index, rows):
    return pl.ds(pl.multiple_of(index * rows, rows), rows)


def split_kernel(order_ref, k_ref, v_ref, early_ref, late_ref):
    rows = early_ref.shape[0]
    width = k_ref.shape[1]
    flip = flip_of(order_ref)
    for out, index in ((early_ref, flip), (late_ref, 1 - flip)):
        out[:, :width] = k_ref[half(index, rows), :]
        out[:, width:] = v_ref[half(index, rows), :]


def split_halves(order, keys, values):
    rows, width = keys.shape[0] // 2, keys.shape[1]
    out = jax.ShapeDtypeStruct((rows, 2 * width), keys.dtype)
    return pl.pallas_call(
        split_kernel,
        out_shape=(out, out),
        in_specs=[whole(SMEM), whole(VMEM), whole(VMEM)],
        out_specs=(whole(VMEM), whole(VMEM)),
        compiler_params=params(),
        name="split_halves",
        cost_estimate=cost(1000, 1 << 20),
    )(order, keys, values)


def attend(q_rows, pieces, biases, diagonal, kv_heads):
    rows = q_rows.shape[0]
    width = kv_heads * HEAD_SIZE
    group = q_rows.shape[1] // width
    factor = HEAD_SIZE ** (-0.5) * math.log2(math.e)
    outs = []
    for h in range(kv_heads):
        lanes = slice(h * HEAD_SIZE, (h + 1) * HEAD_SIZE)
        v_lanes = slice(width + h * HEAD_SIZE, width + (h + 1) * HEAD_SIZE)
        keys = jnp.concatenate([p[:, lanes] for p in pieces], axis=0)
        vals = jnp.concatenate([p[:, v_lanes] for p in pieces], axis=0)
        heads = [
            q_rows[:, (h * group + g) * HEAD_SIZE : (h * group + g + 1) * HEAD_SIZE]
            for g in range(group)
        ]
        stacked = jnp.concatenate(heads, axis=0)
        scores = lax.dot_general(
            stacked, keys, (((1,), (1,)), ((), ())), preferred_element_type=jnp.float32
        )
        parts = []
        for j, bias in enumerate(biases):
            part = scores[:, j * rows : (j + 1) * rows]
            if bias is not None:
                part = part + bias
            parts.append(part)
        last = scores[:, len(biases) * rows :].reshape(group, rows, rows)
        parts.append(jnp.where(diagonal[None], last, FAR).reshape(group * rows, rows))
        peak = functools.reduce(jnp.maximum, parts)
        peak = jnp.max(peak, axis=1, keepdims=True)
        weights = [jnp.exp2((part - peak) * factor) for part in parts]
        total = jnp.sum(functools.reduce(jnp.add, weights), axis=1, keepdims=True)
        rounded = jnp.concatenate([w.astype(jnp.bfloat16) for w in weights], axis=1)
        mixed = lax.dot_general(
            rounded, vals, (((1,), (0,)), ((), ())), preferred_element_type=jnp.float32
        )
        mixed = (mixed / total).astype(jnp.bfloat16)
        outs += [mixed[g * rows : (g + 1) * rows] for g in range(group)]
    return jnp.concatenate(outs, axis=1)


def project(att, w_ref, away_ref, keep_ref, n_core):
    head = lax.axis_index("head")
    chip, core = head // n_core, head % n_core
    cols = away_ref.shape[1] // 2
    for i, owner_chip in enumerate((1 - chip, chip)):
        for ref, owner_core in ((away_ref, 1 - core), (keep_ref, core)):
            start = pl.multiple_of((owner_chip * n_core + owner_core) * cols, cols)
            block = jnp.dot(att, w_ref[:, pl.ds(start, cols)], preferred_element_type=jnp.float32)
            ref[:, i * cols : (i + 1) * cols] = block.astype(ref.dtype)


def side_kernel(late, kv_heads, n_core, order_ref, q_ref, w_ref, *refs):
    *piece_refs, away_ref, keep_ref = refs
    rows = away_ref.shape[0]
    me = lax.axis_index("seq")
    mine = early_of(order_ref, me)
    flip = flip_of(order_ref)
    q_rows = q_ref[half((1 - flip) if late else flip, rows), :]
    peers = [early_of(order_ref, me ^ p) for p in (1, 2, 3)]
    if late:
        biases = [None] * 4 + [jnp.where(c > mine, 0.0, FAR) for c in peers]
    else:
        biases = [jnp.where(c < mine, 0.0, FAR) for c in peers]
    row = lax.broadcasted_iota(jnp.int32, (rows, rows), 0)
    col = lax.broadcasted_iota(jnp.int32, (rows, rows), 1)
    att = attend(q_rows, [r[...] for r in piece_refs], biases, col <= row, kv_heads)
    project(att, w_ref, away_ref, keep_ref, n_core)


def side(late, kv_heads, n_core, order, queries, weight, pieces):
    rows, depth = queries.shape[0] // 2, queries.shape[1]
    cols = weight.shape[1] // 2
    keys = rows * len(pieces)
    flops = 4 * rows * depth * keys + 2 * rows * depth * weight.shape[1]
    return pl.pallas_call(
        functools.partial(side_kernel, late, kv_heads, n_core),
        out_shape=(
            jax.ShapeDtypeStruct((rows, cols), jnp.bfloat16),
            jax.ShapeDtypeStruct((rows, cols), jnp.float32),
        ),
        in_specs=[whole(SMEM)] + [whole(VMEM)] * (2 + len(pieces)),
        out_specs=(whole(VMEM), whole(VMEM)),
        compiler_params=params(),
        name="late_side" if late else "early_side",
        cost_estimate=cost(flops, 16 << 20, rows * depth * keys // HEAD_SIZE),
    )(order, queries, weight, *pieces)


def load_kernel(w_ref, out_ref, sem):
    copy = pltpu.make_async_copy(w_ref, out_ref, sem)
    copy.start()
    copy.wait()


def load_weights(weight):
    return pl.pallas_call(
        load_kernel,
        out_shape=vmem_out(weight.shape, weight.dtype),
        in_specs=[whole(pl.ANY)],
        out_specs=whole(VMEM),
        scratch_shapes=[pltpu.SemaphoreType.DMA],
        compiler_params=pltpu.CompilerParams(vmem_limit_bytes=12 * 2**20),
        name="load_weights",
        cost_estimate=cost(1 << 20, 16 << 20),
    )(weight)


def mix_kernel(late, order_ref, res_ref, keep_ref, core_ref, chip_ref, mixed_ref, sq_ref):
    rows = mixed_ref.shape[0]
    cols = mixed_ref.shape[1]
    flip = flip_of(order_ref)
    res = res_ref[half((1 - flip) if late else flip, rows), :].astype(jnp.float32)
    own = keep_ref[:, cols:] + core_ref[:, cols:].astype(jnp.float32)
    mixed = res + (own + chip_ref[...].astype(jnp.float32))
    mixed_ref[...] = mixed
    squares = mixed * mixed
    lanes = functools.reduce(
        jnp.add, [squares[:, j : j + rows] for j in range(0, cols, rows)]
    )
    sq_ref[...] = jnp.broadcast_to(jnp.sum(lanes.T, axis=0, keepdims=True), sq_ref.shape)


def mix(late, order, residual, keep, core, chip):
    rows, cols = residual.shape[0] // 2, residual.shape[1]
    return pl.pallas_call(
        functools.partial(mix_kernel, late),
        out_shape=(
            jax.ShapeDtypeStruct((rows, cols), jnp.float32),
            jax.ShapeDtypeStruct((8, rows), jnp.float32),
        ),
        in_specs=[whole(SMEM)] + [whole(VMEM)] * 4,
        out_specs=(whole(VMEM), whole(VMEM)),
        compiler_params=params(),
        name="late_mix" if late else "early_mix",
        cost_estimate=cost(1 << 20, 2 << 20),
    )(order, residual, keep, core, chip)


def final_kernel(features, order_ref, gain_ref, early_ref, late_ref, *refs):
    *sq_refs, out_ref = refs
    rows, cols = early_ref.shape
    flip = flip_of(order_ref)
    gain = gain_ref[...].astype(jnp.float32)
    totals = functools.reduce(jnp.add, [r[...] for r in sq_refs])
    for i, (ref, index) in enumerate(((early_ref, flip), (late_ref, 1 - flip))):
        inverse = lax.rsqrt(totals[8 * i : 8 * i + 1] / features + norm_epsilon)
        inverse = jnp.broadcast_to(inverse, (rows, rows)).T
        for j in range(0, cols, rows):
            block = ref[:, j : j + rows] * inverse * gain[:, j : j + rows]
            out_ref[half(index, rows), j : j + rows] = block.astype(out_ref.dtype)


def final(features, order, gain, early, late, sums):
    rows, cols = early.shape
    return pl.pallas_call(
        functools.partial(final_kernel, features),
        out_shape=jax.ShapeDtypeStruct((2 * rows, cols), jnp.bfloat16),
        in_specs=[whole(SMEM)] + [whole(VMEM)] * (3 + len(sums)),
        out_specs=whole(VMEM),
        compiler_params=params(),
        name="final_norm",
        cost_estimate=cost(1 << 20, 2 << 20),
    )(order, gain.reshape(1, cols), early, late, *sums)


def exchange(x, axis, size, step):
    return lax.ppermute(x, axis, [(i, i ^ step) for i in range(size)])


def paired_body(n_seq, n_head, n_core, queries, keys, values, residual, weight, gain, order):
    kv_heads = keys.shape[1] // HEAD_SIZE
    cols = residual.shape[1]
    early, late = split_halves(order, keys, values)
    seq = lambda x, step: exchange(x, "seq", n_seq, step)
    head = lambda x, step: exchange(x, "head", n_head, step)

    early_b = seq(early, 2)
    early_a = seq(early, 1)
    late_b = seq(late, 2)
    early_c = seq(early_b, 1)
    late_a = seq(late, 1)
    late_c = seq(late_b, 1)
    held = load_weights(weight)

    away_e, keep_e = side(
        False, kv_heads, n_core, order, queries, held, [early_a, early_b, early_c, early]
    )
    core_e = head(away_e, 1)
    chip_e = head((keep_e[:, :cols] + core_e[:, :cols].astype(jnp.float32)).astype(jnp.bfloat16), n_core)

    away_l, keep_l = side(
        True,
        kv_heads,
        n_core,
        order,
        queries,
        held,
        [early, early_a, early_b, early_c, late_a, late_b, late_c, late],
    )
    core_l = head(away_l, 1)
    chip_l = head((keep_l[:, :cols] + core_l[:, :cols].astype(jnp.float32)).astype(jnp.bfloat16), n_core)

    mixed_e, sq_e = mix(False, order, residual, keep_e, core_e, chip_e)
    mixed_l, sq_l = mix(True, order, residual, keep_l, core_l, chip_l)
    own = jnp.concatenate([sq_e, sq_l], axis=0)
    others = [head(own, step) for step in range(1, n_head)]
    return final(n_head * cols, order, gain, mixed_e, mixed_l, [own] + others)


def slot_positions(row_ids, block_order, block_rows):
    slot_index = row_ids // block_rows
    slot_ids = jnp.arange(block_order.shape[0], dtype=jnp.int32)
    starts = jnp.sum(
        jnp.where(slot_index[:, None] == slot_ids[None, :], block_order[None, :], 0), axis=1
    )
    return starts * block_rows + row_ids % block_rows


def attend_block(carried, query_rows, query_positions, key_block, value_block, key_positions):
    row_peak, denominators, weighted_sum = carried
    scores = jnp.einsum(
        "qhgd,khd->hgqk", query_rows, key_block, preferred_element_type=jnp.float32
    ) * HEAD_SIZE ** (-0.5)
    visible = (key_positions[None, :] <= query_positions[:, None])[None, None]
    scores = jnp.where(visible, scores, FAR)
    new_peak = jnp.maximum(row_peak, jnp.max(scores, axis=3))
    weights = jnp.where(visible, jnp.exp(scores - new_peak[..., None]), 0.0)
    factor = jnp.exp(row_peak - new_peak)
    denominators = denominators * factor + jnp.sum(weights, axis=3)
    weighted_sum = weighted_sum * factor[..., None] + jnp.einsum(
        "hgqk,khd->hgqd",
        weights.astype(jnp.bfloat16),
        value_block,
        preferred_element_type=jnp.float32,
    )
    return (new_peak, denominators, weighted_sum)


def gathered_body(n_head, queries, keys, values, residual, weight, gain, order):
    tok_rows = queries.shape[0]
    block_rows = tok_rows // 2
    kv_heads = keys.shape[1] // HEAD_SIZE
    q_heads = queries.shape[1] // HEAD_SIZE
    group = q_heads // kv_heads
    own_rows = lax.axis_index("seq") * tok_rows + jnp.arange(tok_rows, dtype=jnp.int32)
    own_positions = slot_positions(own_rows, order, block_rows)
    shaped = queries.reshape(tok_rows, kv_heads, group, HEAD_SIZE)
    all_keys = lax.all_gather(keys, "seq", axis=0, tiled=True)
    all_values = lax.all_gather(values, "seq", axis=0, tiled=True)
    count = all_keys.shape[0]
    width = math.gcd(count, 512)
    all_keys = all_keys.reshape(count, kv_heads, HEAD_SIZE)
    all_values = all_values.reshape(count, kv_heads, HEAD_SIZE)

    def one_step(index, state):
        offset = index * width
        row_ids = offset + jnp.arange(width, dtype=jnp.int32)
        return attend_block(
            state,
            shaped,
            own_positions,
            lax.dynamic_slice_in_dim(all_keys, offset, width, 0),
            lax.dynamic_slice_in_dim(all_values, offset, width, 0),
            slot_positions(row_ids, order, block_rows),
        )

    state = (
        jnp.full((kv_heads, group, tok_rows), FAR, jnp.float32),
        jnp.zeros((kv_heads, group, tok_rows), jnp.float32),
        jnp.zeros((kv_heads, group, tok_rows, HEAD_SIZE), jnp.float32),
    )
    _, denominators, weighted_sum = lax.fori_loop(0, count // width, one_step, state)
    att = (weighted_sum / denominators[..., None]).transpose(2, 0, 1, 3)
    att = att.reshape(tok_rows, q_heads * HEAD_SIZE).astype(jnp.bfloat16)
    partial_terms = jnp.dot(att, weight, preferred_element_type=jnp.float32)
    projected = lax.psum_scatter(
        partial_terms.astype(jnp.bfloat16), "head", scatter_dimension=1, tiled=True
    ).astype(jnp.float32)
    mixed = residual.astype(jnp.float32) + projected
    totals = lax.psum(jnp.sum(mixed * mixed, axis=1), "head")
    inverse = lax.rsqrt(totals / (n_head * residual.shape[1]) + norm_epsilon)
    return (mixed * inverse[:, None] * gain.astype(jnp.float32)[None, :]).astype(jnp.bfloat16)


def solution(mesh):
    n_seq, n_head = mesh.shape["seq"], mesh.shape["head"]
    rows, wide = P(("rep", "seq"), "head"), P("head", None)
    in_specs = (rows, rows, rows, rows, wide, P("head"), P("rep"))
    if n_seq == 4 and n_head == 4:
        body = functools.partial(paired_body, n_seq, n_head, n_head // 2)
    else:
        body = functools.partial(gathered_body, n_head)
    return jax.shard_map(body, mesh=mesh, in_specs=in_specs, out_specs=rows, check_vma=False)
```

time: 113 us -> 54 us (0.48)
  blocking collectives: 40.2 us -> 0 us
  starting transfers between devices: 0.01 us -> 13.9 us
  between operations: 13.5 us -> 0.14 us
  matrix products: 13.2 us -> 0 us
  Pallas kernels: 0 us -> 10.7 us
  waiting for transfers between devices: 31.1 us -> 22.8 us
  other arithmetic: 6.97 us -> 0.14 us
    all_gather x2 -> x0, blocking collectives: 34.5 us -> none  [the longest x1 17.4 us: body(): key_piece = lax.all_gather(rotated_key_states, 'seq', axis=0, tiled=True)]
    reduce_scatter x1 -> x0, waiting for transfers between devices: 31.1 us -> none  [body(): lax.psum_scatter(partial_terms.astype(jnp.bfloat16), 'head', scatter_dime...]
    ppermute x0 -> x13, waiting for transfers between devices: none -> 22.8 us  [exchange(): return lax.ppermute(x, axis, [(i, i ^ step) for i in range(size)])]
    ppermute x0 -> x13, starting transfers between devices: none -> 13.9 us  [exchange(): return lax.ppermute(x, axis, [(i, i ^ step) for i in range(size)])]
    dot_general x9 -> x0, matrix products: 13.2 us -> none  [the longest x1 7.11 us: body(): jnp.dot(attention, out_weight, preferred_element_type=jnp.float32)]
    pallas_call x0 -> x7, Pallas kernels: none -> 10.7 us  [the longest x2 6.47 us: side(): pl.pallas_call(functools.partial(side_kernel, late, kv_heads, n_core), ou...]
    psum x1 -> x0, blocking collectives: 5.76 us -> none  [body(): totals = lax.psum(squares, 'head')]
    unnamed x16 -> x17, local copies, waits for them, and re-layouts: 1.57 us -> 6.14 us
  transfers between devices with their start and end apart: 1 -> 13, of which waited for: 1 -> 7; matrix products, arithmetic and copies ran while one was open for 0% -> 0% of each run, Pallas kernels for 0% -> 15%
where the time goes in v1:
time: 54 us; the launch traced here: 53.8 us
  waiting for transfers between devices  22.8 us (42%)
  starting transfers between devices  13.9 us (26%)
  Pallas kernels  10.7 us (20%)
  local copies, waits for them, and re-layouts  6.15 us (11%)
    ppermute x13, waiting for transfers between devices, exchange(): return lax.ppermute(x, axis, [(i, i ^ step) for i in range(size)])  22.8 us
    ppermute x13, starting transfers between devices, exchange(): return lax.ppermute(x, axis, [(i, i ^ step) for i in range(size)])  13.9 us
    pallas_call x2, Pallas kernels, side(): pl.pallas_call(functools.partial(side_kernel, late, kv_heads, n_core), ou...  6.47 us
    unnamed x17, local copies, waits for them, and re-layouts  6.14 us
    pallas_call x1, Pallas kernels, final(): pl.pallas_call(functools.partial(final_kernel, features), out_shape=jax.S...  1.53 us
    pallas_call x2, Pallas kernels, mix(): pl.pallas_call(functools.partial(mix_kernel, late), out_shape=(jax.ShapeD...  1.53 us
  transfers between devices with their start and end apart: 13, of which 7 were waited for; matrix products, arithmetic and copies ran while one was open for 0% of the time, Pallas kernels for 15%

profile of v1, /device:TPU:0, one launch (start us, length us, event | category | flops | bytes accessed | tf_op | source)
XLA Modules:
  0.0 53.8 jit_solution(4383857335560522587)
XLA Ops:
  0.0 0.0 copy-start.3
  0.0 0.9 %copy-done.3 = bf16[256,256]{1,0:T(8,128)(2,1)S(1)} copy-done((bf16[256,256]{1,0:T(8,128)(2,1)S(1)}, bf16[256,256]{1,0:T(8,128)(2,1)}, u32[]{:S(2)}) %copy-start.3) | copy-done | bytes 131096
  0.9 0.0 copy-start.4
  0.9 0.9 %copy-done.4 = bf16[256,256]{1,0:T(8,128)(2,1)S(1)} copy-done((bf16[256,256]{1,0:T(8,128)(2,1)S(1)}, bf16[256,256]{1,0:T(8,128)(2,1)}, u32[]{:S(2)}) %copy-start.4) | copy-done | bytes 131096
  1.8 0.0 copy-start.5
  1.8 0.7 %copy-done.5 = s32[8]{0:T(128)S(1)} copy-done((s32[8]{0:T(128)S(1)}, s32[8]{0:T(128)}, u32[]{:S(2)}) %copy-start.5) | copy-done | bytes 56
  2.5 0.6 %split_halves.1 = (bf16[128,512]{1,0:T(8,128)(2,1)S(1)}, bf16[128,512]{1,0:T(8,128)(2,1)S(1)}) custom-call(s32[8]{0:T(128)S(1)} %copy-done.5, bf16[256,256]{1,0:T(8,128)(2,1)S(1)} %copy-done.3, bf16[256,256]{1,0:T(8,128)(2,1)S(1)} %copy-done.4), custom_call_target="tpu_custom_call" | custom-call | flops 1000 | bytes 1048576 | tf_op jit(solution)/shard_map/split_halves/pallas_call | solution.py:60
  3.0 4.1 %collective-permute-start.1 = (bf16[128,512]{1,0:T(8,128)(2,1)S(1)}, bf16[128,512]{1,0:T(8,128)(2,1)S(1)}, u32[]{:S(2)}, u32[]{:S(2)}) collective-permute-start(bf16[128,512]{1,0:T(8,128)(2,1)S(1)} %get-tuple-element.15.refs_3_.refs_0_), channel_id=1, source_target_pairs={{0,8},{4,12},{8,0},{12,4},{1,9},{5,13},{9,1},{13,5},{2,10},{6,14},... | collective-permute-start | bytes 393224 | tf_op jit(solution)/shard_map/ppermute | solution.py:237
  7.2 0.1 collective-permute-start.6
  7.3 1.8 %collective-permute-start = (bf16[128,512]{1,0:T(8,128)(2,1)S(1)}, bf16[128,512]{1,0:T(8,128)(2,1)S(1)}, u32[]{:S(2)}, u32[]{:S(2)}) collective-permute-start(bf16[128,512]{1,0:T(8,128)(2,1)S(1)} %get-tuple-element.15.refs_3_.refs_0_), channel_id=1, source_target_pairs={{0,4},{4,0},{8,12},{12,8},{1,5},{5,1},{9,13},{13,9},{2,6},{6,2},{1... | collective-permute-start | bytes 393224 | tf_op jit(solution)/shard_map/ppermute | solution.py:237
  9.1 8.0 %collective-permute-done.1.refs_1_.refs_2_ = bf16[128,512]{1,0:T(8,128)(2,1)S(1)} collective-permute-done((bf16[128,512]{1,0:T(8,128)(2,1)S(1)}, bf16[128,512]{1,0:T(8,128)(2,1)S(1)}, u32[]{:S(2)}, u32[]{:S(2)}) %collective-permute-start.1) | collective-permute-done | bytes 131104 | tf_op jit(solution)/shard_map/ppermute | solution.py:237
  17.1 0.0 collective-permute-start.2
  17.1 2.0 %collective-permute-start.5 = (bf16[128,512]{1,0:T(8,128)(2,1)S(1)}, bf16[128,512]{1,0:T(8,128)(2,1)S(1)}, u32[]{:S(2)}, u32[]{:S(2)}) collective-permute-start(bf16[128,512]{1,0:T(8,128)(2,1)S(1)} %get-tuple-element.19.refs_7_), channel_id=1, source_target_pairs={{0,4},{4,0},{8,12},{12,8},{1,5},{5,1},{9,13},{13,9},{2,6},{6,2},{1... | collective-permute-start | bytes 393224 | tf_op jit(solution)/shard_map/ppermute | solution.py:237
  19.2 3.4 %copy-done = bf16[1024,4096]{1,0:T(8,128)(2,1)S(1)} copy-done((bf16[1024,4096]{1,0:T(8,128)(2,1)S(1)}, bf16[1024,4096]{1,0:T(8,128)(2,1)}, u32[]{:S(2)}) %copy-start) | copy-done | bytes 8388632
  22.6 0.6 %load_weights.1.w_ref = bf16[1024,4096]{1,0:T(8,128)(2,1)S(1)} custom-call(bf16[1024,4096]{1,0:T(8,128)(2,1)S(1)} %copy-done), custom_call_target="tpu_custom_call" | custom-call | flops 1048576 | bytes 16777216 | tf_op jit(solution)/shard_map/load_weights/pallas_call | solution.py:166
  23.1 0.0 collective-permute-done.6.refs_5_
  23.1 0.1 collective-permute-start.7
  23.2 0.0 collective-permute-done.refs_0_.refs_1_
  23.2 0.1 collective-permute-done.2.refs_2_.refs_3_
  23.3 0.0 copy-done.6
  23.3 0.3 copy-done.1
  23.6 2.8 %early_side.1 = (bf16[128,2048]{1,0:T(8,128)(2,1)S(1)}, f32[128,2048]{1,0:T(8,128)S(1)}) custom-call(s32[8]{0:T(128)S(1)} %copy-done.6, bf16[256,1024]{1,0:T(8,128)(2,1)S(1)} %copy-done.1, bf16[1024,4096]{1,0:T(8,128)(2,1)S(1)} %load_weights.1.w_ref, bf16[128,512]{1,0:T(8,128)(2,1)S(1)} %collective-permute-done.refs_0_.refs_1_, ...), custom_call_target="tpu_custom_call" | custom-call | flops 1342177280 | bytes 16777216 | tf_op jit(solution)/shard_map/early_side/pallas_call | solution.py:145
  26.4 0.0 copy-start.2
  26.4 0.0 copy-start.7
  26.4 0.1 collective-permute-start.3
  26.5 0.0 collective-permute-done.5.refs_4_
  26.5 1.7 %collective-permute-done.7.refs_6_ = bf16[128,512]{1,0:T(8,128)(2,1)S(1)} collective-permute-done((bf16[128,512]{1,0:T(8,128)(2,1)S(1)}, bf16[128,512]{1,0:T(8,128)(2,1)S(1)}, u32[]{:S(2)}, u32[]{:S(2)}) %collective-permute-start.7) | collective-permute-done | bytes 131104 | tf_op jit(solution)/shard_map/ppermute | solution.py:237
  28.2 3.7 %late_side.1 = (bf16[128,2048]{1,0:T(8,128)(2,1)S(1)}, f32[128,2048]{1,0:T(8,128)S(1)}) custom-call(s32[8]{0:T(128)S(1)} %copy-done.6, bf16[256,1024]{1,0:T(8,128)(2,1)S(1)} %copy-done.1, bf16[1024,4096]{1,0:T(8,128)(2,1)S(1)} %load_weights.1.w_ref, bf16[128,512]{1,0:T(8,128)(2,1)S(1)} %get-tuple-element.15.refs_3_.refs_0_, ...), custom_call_target="tpu_custom_call" | custom-call | flops 1610612736 | bytes 16777216 | tf_op jit(solution)/shard_map/late_side/pallas_call | solution.py:145
  31.9 0.1 collective-permute-start.8
  32.0 0.0 collective-permute-done.3.core_ref
  32.0 0.1 add_convert_fusion.1
  32.1 1.9 %collective-permute-start.4 = (bf16[128,1024]{1,0:T(8,128)(2,1)S(1)}, bf16[128,1024]{1,0:T(8,128)(2,1)S(1)}, u32[]{:S(2)}, u32[]{:S(2)}) collective-permute-start(bf16[128,1024]{1,0:T(8,128)(2,1)S(1)} %add_convert_fusion.1), channel_id=1, source_target_pairs={{0,2},{1,3},{2,0},{3,1},{4,6},{5,7},{6,4},{7,5},{8,10},{9,11},{10,... | collective-permute-start | bytes 786440 | tf_op jit(solution)/shard_map/ppermute | solution.py:237
  33.9 0.0 collective-permute-done.8.core_ref
  33.9 0.1 add_convert_fusion
  34.0 1.8 %collective-permute-start.9 = (bf16[128,1024]{1,0:T(8,128)(2,1)S(1)}, bf16[128,1024]{1,0:T(8,128)(2,1)S(1)}, u32[]{:S(2)}, u32[]{:S(2)}) collective-permute-start(bf16[128,1024]{1,0:T(8,128)(2,1)S(1)} %add_convert_fusion), channel_id=1, source_target_pairs={{0,2},{1,3},{2,0},{3,1},{4,6},{5,7},{6,4},{7,5},{8,10},{9,11},{10,... | collective-permute-start | bytes 786440 | tf_op jit(solution)/shard_map/ppermute | solution.py:237
  35.8 5.5 %collective-permute-done.4.chip_ref = bf16[128,1024]{1,0:T(8,128)(2,1)S(1)} collective-permute-done((bf16[128,1024]{1,0:T(8,128)(2,1)S(1)}, bf16[128,1024]{1,0:T(8,128)(2,1)S(1)}, u32[]{:S(2)}, u32[]{:S(2)}) %collective-permute-start.4) | collective-permute-done | bytes 262176 | tf_op jit(solution)/shard_map/ppermute | solution.py:237
  41.3 0.0 copy-done.2
  41.3 0.8 %early_mix.1 = (f32[128,1024]{1,0:T(8,128)S(1)}, f32[8,128]{1,0:T(8,128)S(1)}) custom-call(s32[8]{0:T(128)S(1)} %copy-done.6, bf16[256,1024]{1,0:T(8,128)(2,1)S(1)} %copy-done.2, f32[128,2048]{1,0:T(8,128)S(1)} %get-tuple-element.16.keep_ref, bf16[128,2048]{1,0:T(8,128)(2,1)S(1)} %collective-permute-done.3.core_ref, ...), custom_call_target="tpu_custom_call" | custom-call | flops 1048576 | bytes 2097152 | tf_op jit(solution)/shard_map/early_mix/pallas_call | solution.py:195
  42.1 4.4 %collective-permute-done.9.chip_ref = bf16[128,1024]{1,0:T(8,128)(2,1)S(1)} collective-permute-done((bf16[128,1024]{1,0:T(8,128)(2,1)S(1)}, bf16[128,1024]{1,0:T(8,128)(2,1)S(1)}, u32[]{:S(2)}, u32[]{:S(2)}) %collective-permute-start.9) | collective-permute-done | bytes 262176 | tf_op jit(solution)/shard_map/ppermute | solution.py:237
  46.5 0.8 %late_mix.1 = (f32[128,1024]{1,0:T(8,128)S(1)}, f32[8,128]{1,0:T(8,128)S(1)}) custom-call(s32[8]{0:T(128)S(1)} %copy-done.6, bf16[256,1024]{1,0:T(8,128)(2,1)S(1)} %copy-done.2, f32[128,2048]{1,0:T(8,128)S(1)} %get-tuple-element.20.keep_ref, bf16[128,2048]{1,0:T(8,128)(2,1)S(1)} %collective-permute-done.8.core_ref, ...), custom_call_target="tpu_custom_call" | custom-call | flops 1048576 | bytes 2097152 | tf_op jit(solution)/shard_map/late_mix/pallas_call | solution.py:195
  47.3 0.1 collective-permute-start.10
  47.4 1.8 %collective-permute-start.11 = (f32[16,128]{1,0:T(8,128)S(1)}, f32[16,128]{1,0:T(8,128)S(1)}, u32[]{:S(2)}, u32[]{:S(2)}) collective-permute-start(f32[16,128]{1,0:T(8,128)S(1)} %constant_dynamic-update-slice_fusion.refs_0_), channel_id=1, source_target_pairs={{0,2},{1,3},{2,0},{3,1},{4,6},{5,7},{6,4},{7,5},{8,10},{9,11},{10,... | collective-permute-start | bytes 24584 | tf_op jit(solution)/shard_map/ppermute | solution.py:237
  49.2 0.0 collective-permute-start.12
  49.2 0.0 copy-done.7
  49.2 0.0 collective-permute-done.10.refs_1_
  49.2 1.9 %collective-permute-done.11.refs_2_ = f32[16,128]{1,0:T(8,128)S(1)} collective-permute-done((f32[16,128]{1,0:T(8,128)S(1)}, f32[16,128]{1,0:T(8,128)S(1)}, u32[]{:S(2)}, u32[]{:S(2)}) %collective-permute-start.11) | collective-permute-done | bytes 8224 | tf_op jit(solution)/shard_map/ppermute | solution.py:237
  51.1 1.2 %collective-permute-done.12.refs_3_ = f32[16,128]{1,0:T(8,128)S(1)} collective-permute-done((f32[16,128]{1,0:T(8,128)S(1)}, f32[16,128]{1,0:T(8,128)S(1)}, u32[]{:S(2)}, u32[]{:S(2)}) %collective-permute-start.12) | collective-permute-done | bytes 8224 | tf_op jit(solution)/shard_map/ppermute | solution.py:237
  52.2 1.5 %final_norm.1 = bf16[256,1024]{1,0:T(8,128)(2,1)} custom-call(s32[8]{0:T(128)S(1)} %copy-done.6, bf16[1,1024]{1,0:T(2,128)(2,1)S(1)} %reshape.3.gain_ref, f32[128,1024]{1,0:T(8,128)S(1)} %get-tuple-element.18.early_ref, f32[128,1024]{1,0:T(8,128)S(1)} %get-tuple-element.22.late_ref, f32[16,128]{1,0:T(8,128)S(1)} %constant_dynamic-update-slice_fusion.refs_0_, ...), custom_call_target="tpu_custom_call" | custom-call | flops 1048576 | bytes 2097152 | tf_op jit(solution)/shard_map/final_norm/pallas_call | solution.py:225
  (6 shorter events, 0.0 us)
Async XLA Ops:
  0.0 0.9 %copy-start.3 = (bf16[256,256]{1,0:T(8,128)(2,1)S(1)}, bf16[256,256]{1,0:T(8,128)(2,1)}, u32[]{:S(2)}) copy-start(bf16[256,256]{1,0:T(8,128)(2,1)} %k_ref.1) | copy-start | bytes 393220
  0.9 0.9 %copy-start.4 = (bf16[256,256]{1,0:T(8,128)(2,1)S(1)}, bf16[256,256]{1,0:T(8,128)(2,1)}, u32[]{:S(2)}) copy-start(bf16[256,256]{1,0:T(8,128)(2,1)} %v_ref.1) | copy-start | bytes 393220
  1.8 0.7 %copy-start.5 = (s32[8]{0:T(128)S(1)}, s32[8]{0:T(128)}, u32[]{:S(2)}) copy-start(s32[8]{0:T(128)} %order_ref.11) | copy-start | bytes 100
  3.0 14.1 %collective-permute-start.1 = (bf16[128,512]{1,0:T(8,128)(2,1)S(1)}, bf16[128,512]{1,0:T(8,128)(2,1)S(1)}, u32[]{:S(2)}, u32[]{:S(2)}) collective-permute-start(bf16[128,512]{1,0:T(8,128)(2,1)S(1)} %get-tuple-element.15.refs_3_.refs_0_), channel_id=1, source_target_pairs={{0,8},{4,12},{8,0},{12,4},{1,9},{5,13},{9,1},{13,5},{2,10},{6,14},... | collective-permute-start | bytes 393224 | tf_op jit(solution)/shard_map/ppermute | solution.py:237
  7.2 16.1 %copy-start.6 = (s32[8]{0:T(128)S(1)}, s32[8]{0:T(128)}, u32[]{:S(2)}) copy-start(s32[8]{0:T(128)} %order_ref.11) | copy-start | bytes 100
  7.2 16.0 %collective-permute-start.6 = (bf16[128,512]{1,0:T(8,128)(2,1)S(1)}, bf16[128,512]{1,0:T(8,128)(2,1)S(1)}, u32[]{:S(2)}, u32[]{:S(2)}) collective-permute-start(bf16[128,512]{1,0:T(8,128)(2,1)S(1)} %get-tuple-element.19.refs_7_), channel_id=1, source_target_pairs={{0,8},{4,12},{8,0},{12,4},{1,9},{5,13},{9,1},{13,5},{2,10},{6,14},... | collective-permute-start | bytes 393224 | tf_op jit(solution)/shard_map/ppermute | solution.py:237
  7.3 16.0 %collective-permute-start = (bf16[128,512]{1,0:T(8,128)(2,1)S(1)}, bf16[128,512]{1,0:T(8,128)(2,1)S(1)}, u32[]{:S(2)}, u32[]{:S(2)}) collective-permute-start(bf16[128,512]{1,0:T(8,128)(2,1)S(1)} %get-tuple-element.15.refs_3_.refs_0_), channel_id=1, source_target_pairs={{0,4},{4,0},{8,12},{12,8},{1,5},{5,1},{9,13},{13,9},{2,6},{6,2},{1... | collective-permute-start | bytes 393224 | tf_op jit(solution)/shard_map/ppermute | solution.py:237
  17.1 6.2 %collective-permute-start.2 = (bf16[128,512]{1,0:T(8,128)(2,1)S(1)}, bf16[128,512]{1,0:T(8,128)(2,1)S(1)}, u32[]{:S(2)}, u32[]{:S(2)}) collective-permute-start(bf16[128,512]{1,0:T(8,128)(2,1)S(1)} %collective-permute-done.1.refs_1_.refs_2_), channel_id=1, source_target_pairs={{0,4},{4,0},{8,12},{12,8},{1,5},{5,1},{9,13},{13,9},{2,6},{6,2},{1... | collective-permute-start | bytes 393224 | tf_op jit(solution)/shard_map/ppermute | solution.py:237
  17.1 9.3 %collective-permute-start.5 = (bf16[128,512]{1,0:T(8,128)(2,1)S(1)}, bf16[128,512]{1,0:T(8,128)(2,1)S(1)}, u32[]{:S(2)}, u32[]{:S(2)}) collective-permute-start(bf16[128,512]{1,0:T(8,128)(2,1)S(1)} %get-tuple-element.19.refs_7_), channel_id=1, source_target_pairs={{0,4},{4,0},{8,12},{12,8},{1,5},{5,1},{9,13},{13,9},{2,6},{6,2},{1... | collective-permute-start | bytes 393224 | tf_op jit(solution)/shard_map/ppermute | solution.py:237
  19.2 3.4 %copy-start = (bf16[1024,4096]{1,0:T(8,128)(2,1)S(1)}, bf16[1024,4096]{1,0:T(8,128)(2,1)}, u32[]{:S(2)}) copy-start(bf16[1024,4096]{1,0:T(8,128)(2,1)} %w_ref.1) | copy-start | bytes 25165828
  22.6 1.0 %copy-start.1 = (bf16[256,1024]{1,0:T(8,128)(2,1)S(1)}, bf16[256,1024]{1,0:T(8,128)(2,1)}, u32[]{:S(2)}) copy-start(bf16[256,1024]{1,0:T(8,128)(2,1)} %q_ref.3) | copy-start | bytes 1572868
  23.1 5.0 %collective-permute-start.7 = (bf16[128,512]{1,0:T(8,128)(2,1)S(1)}, bf16[128,512]{1,0:T(8,128)(2,1)S(1)}, u32[]{:S(2)}, u32[]{:S(2)}) collective-permute-start(bf16[128,512]{1,0:T(8,128)(2,1)S(1)} %collective-permute-done.6.refs_5_), channel_id=1, source_target_pairs={{0,4},{4,0},{8,12},{12,8},{1,5},{5,1},{9,13},{13,9},{2,6},{6,2},{1... | collective-permute-start | bytes 393224 | tf_op jit(solution)/shard_map/ppermute | solution.py:237
  26.4 15.0 %copy-start.2 = (bf16[256,1024]{1,0:T(8,128)(2,1)S(1)}, bf16[256,1024]{1,0:T(8,128)(2,1)}, u32[]{:S(2)}) copy-start(bf16[256,1024]{1,0:T(8,128)(2,1)} %res_ref.3) | copy-start | bytes 1572868
  26.4 22.8 %copy-start.7 = (bf16[1024]{0:T(1024)(128)(2,1)S(1)}, bf16[1024]{0:T(1024)(128)(2,1)}, u32[]{:S(2)}) copy-start(bf16[1024]{0:T(1024)(128)(2,1)} %param.12) | copy-start | bytes 6148
  26.4 5.6 %collective-permute-start.3 = (bf16[128,2048]{1,0:T(8,128)(2,1)S(1)}, bf16[128,2048]{1,0:T(8,128)(2,1)S(1)}, u32[]{:S(2)}, u32[]{:S(2)}) collective-permute-start(bf16[128,2048]{1,0:T(8,128)(2,1)S(1)} %get-tuple-element.17), channel_id=1, source_target_pairs={{0,1},{1,0},{2,3},{3,2},{4,5},{5,4},{6,7},{7,6},{8,9},{9,8},{10,11... | collective-permute-start | bytes 1572872 | tf_op jit(solution)/shard_map/ppermute | solution.py:237
  31.9 2.0 %collective-permute-start.8 = (bf16[128,2048]{1,0:T(8,128)(2,1)S(1)}, bf16[128,2048]{1,0:T(8,128)(2,1)S(1)}, u32[]{:S(2)}, u32[]{:S(2)}) collective-permute-start(bf16[128,2048]{1,0:T(8,128)(2,1)S(1)} %get-tuple-element.21), channel_id=1, source_target_pairs={{0,1},{1,0},{2,3},{3,2},{4,5},{5,4},{6,7},{7,6},{8,9},{9,8},{10,11... | collective-permute-start | bytes 1572872 | tf_op jit(solution)/shard_map/ppermute | solution.py:237
  32.1 9.2 %collective-permute-start.4 = (bf16[128,1024]{1,0:T(8,128)(2,1)S(1)}, bf16[128,1024]{1,0:T(8,128)(2,1)S(1)}, u32[]{:S(2)}, u32[]{:S(2)}) collective-permute-start(bf16[128,1024]{1,0:T(8,128)(2,1)S(1)} %add_convert_fusion.1), channel_id=1, source_target_pairs={{0,2},{1,3},{2,0},{3,1},{4,6},{5,7},{6,4},{7,5},{8,10},{9,11},{10,... | collective-permute-start | bytes 786440 | tf_op jit(solution)/shard_map/ppermute | solution.py:237
  34.0 12.5 %collective-permute-start.9 = (bf16[128,1024]{1,0:T(8,128)(2,1)S(1)}, bf16[128,1024]{1,0:T(8,128)(2,1)S(1)}, u32[]{:S(2)}, u32[]{:S(2)}) collective-permute-start(bf16[128,1024]{1,0:T(8,128)(2,1)S(1)} %add_convert_fusion), channel_id=1, source_target_pairs={{0,2},{1,3},{2,0},{3,1},{4,6},{5,7},{6,4},{7,5},{8,10},{9,11},{10,... | collective-permute-start | bytes 786440 | tf_op jit(solution)/shard_map/ppermute | solution.py:237
  47.3 1.9 %collective-permute-start.10 = (f32[16,128]{1,0:T(8,128)S(1)}, f32[16,128]{1,0:T(8,128)S(1)}, u32[]{:S(2)}, u32[]{:S(2)}) collective-permute-start(f32[16,128]{1,0:T(8,128)S(1)} %constant_dynamic-update-slice_fusion.refs_0_), channel_id=1, source_target_pairs={{0,1},{1,0},{2,3},{3,2},{4,5},{5,4},{6,7},{7,6},{8,9},{9,8},{10,11... | collective-permute-start | bytes 24584 | tf_op jit(solution)/shard_map/ppermute | solution.py:237
  47.4 3.7 %collective-permute-start.11 = (f32[16,128]{1,0:T(8,128)S(1)}, f32[16,128]{1,0:T(8,128)S(1)}, u32[]{:S(2)}, u32[]{:S(2)}) collective-permute-start(f32[16,128]{1,0:T(8,128)S(1)} %constant_dynamic-update-slice_fusion.refs_0_), channel_id=1, source_target_pairs={{0,2},{1,3},{2,0},{3,1},{4,6},{5,7},{6,4},{7,5},{8,10},{9,11},{10,... | collective-permute-start | bytes 24584 | tf_op jit(solution)/shard_map/ppermute | solution.py:237
  49.2 3.1 %collective-permute-start.12 = (f32[16,128]{1,0:T(8,128)S(1)}, f32[16,128]{1,0:T(8,128)S(1)}, u32[]{:S(2)}, u32[]{:S(2)}) collective-permute-start(f32[16,128]{1,0:T(8,128)S(1)} %constant_dynamic-update-slice_fusion.refs_0_), channel_id=1, source_target_pairs={{0,3},{1,2},{2,1},{3,0},{4,7},{5,6},{6,5},{7,4},{8,11},{9,10},{10,... | collective-permute-start | bytes 24584 | tf_op jit(solution)/shard_map/ppermute | solution.py:237

commit v2 on v1

--- a/solution.py
+++ b/solution.py
@@ -8,16 +8,22 @@
 from jax.experimental.pallas import tpu as pltpu
 from jax.sharding import PartitionSpec as P
 
+
 HEAD_SIZE = 128
 norm_epsilon = 1e-05
 FAR = -1e30
 VMEM = pltpu.VMEM
 SMEM = pltpu.SMEM
+HBM = pltpu.HBM
 LIMIT = 40 * 2**20
 
 
 def vmem_out(shape, dtype):
     return pltpu.VMEM(shape, dtype)
+
+
+def in_hbm(*arrays):
+    return [pltpu.with_memory_space_constraint(x, HBM) for x in arrays]
 
 
 def whole(space):
@@ -45,27 +51,86 @@
     return pl.ds(pl.multiple_of(index * rows, rows), rows)
 
 
-def split_kernel(order_ref, k_ref, v_ref, early_ref, late_ref):
+def split_kernel(order_hbm, k_hbm, v_hbm, early_ref, late_ref, marks_ref, order_ref, kv, sems):
     rows = early_ref.shape[0]
-    width = k_ref.shape[1]
+    width = k_hbm.shape[1]
+    copies = [
+        pltpu.make_async_copy(order_hbm, order_ref, sems.at[0]),
+        pltpu.make_async_copy(k_hbm, kv.at[0], sems.at[1]),
+        pltpu.make_async_copy(v_hbm, kv.at[1], sems.at[2]),
+    ]
+    for copy in copies:
+        copy.start()
+    copies[0].wait()
+    me = lax.axis_index("seq")
+    mine = early_of(order_ref, me)
     flip = flip_of(order_ref)
-    for out, index in ((early_ref, flip), (late_ref, 1 - flip)):
-        out[:, :width] = k_ref[half(index, rows), :]
-        out[:, width:] = v_ref[half(index, rows), :]
+    peers = [early_of(order_ref, me ^ p) for p in (1, 2, 3)]
+    values = [flip.astype(jnp.float32)]
+    values += [jnp.where(c < mine, 0.0, FAR) for c in peers]
+    values += [jnp.where(c > mine, 0.0, FAR) for c in peers]
+    row = lax.broadcasted_iota(jnp.int32, marks_ref.shape, 0)
+    marks = jnp.zeros(marks_ref.shape, jnp.float32)
+    for i, value in enumerate(values):
+        marks = jnp.where(row == i, value, marks)
+    marks_ref[...] = marks
+    for i, copy in enumerate(copies[1:]):
+        copy.wait()
+        lanes = slice(i * width, (i + 1) * width)
+        early_ref[:, lanes] = kv[i, half(flip, rows), :]
+        late_ref[:, lanes] = kv[i, half(1 - flip, rows), :]
 
 
 def split_halves(order, keys, values):
     rows, width = keys.shape[0] // 2, keys.shape[1]
-    out = jax.ShapeDtypeStruct((rows, 2 * width), keys.dtype)
+    out = vmem_out((rows, 2 * width), keys.dtype)
     return pl.pallas_call(
         split_kernel,
-        out_shape=(out, out),
-        in_specs=[whole(SMEM), whole(VMEM), whole(VMEM)],
-        out_specs=(whole(VMEM), whole(VMEM)),
+        out_shape=(out, out, vmem_out((8, HEAD_SIZE), jnp.float32)),
+        in_specs=[whole(HBM)] * 3,
+        out_specs=(whole(VMEM),) * 3,
+        scratch_shapes=[
+            SMEM(order.shape, order.dtype),
+            VMEM((2,) + keys.shape, keys.dtype),
+            pltpu.SemaphoreType.DMA((3,)),
+        ],
         compiler_params=params(),
         name="split_halves",
         cost_estimate=cost(1000, 1 << 20),
-    )(order, keys, values)
+    )(*in_hbm(order, keys, values))
+
+
+def prep_kernel(order_hbm, w_hbm, q_hbm, r_hbm, w_ref, qe_ref, ql_ref, re_ref, rl_ref, order_ref, sems):
+    rows = qe_ref.shape[0]
+    first = pltpu.make_async_copy(order_hbm, order_ref, sems.at[0])
+    first.start()
+    copies = [pltpu.make_async_copy(w_hbm, w_ref, sems.at[1])]
+    copies[0].start()
+    first.wait()
+    flip = flip_of(order_ref)
+    pairs = ((q_hbm, qe_ref, flip), (r_hbm, re_ref, flip), (q_hbm, ql_ref, 1 - flip), (r_hbm, rl_ref, 1 - flip))
+    for i, (source, target, index) in enumerate(pairs):
+        copy = pltpu.make_async_copy(source.at[half(index, rows), :], target, sems.at[2 + i])
+        copy.start()
+        copies.append(copy)
+    for copy in copies:
+        copy.wait()
+
+
+def prep(order, weight, queries, residual):
+    rows, cols = queries.shape[0] // 2, queries.shape[1]
+    part = vmem_out((rows, cols), queries.dtype)
+    other = vmem_out((rows, residual.shape[1]), residual.dtype)
+    return pl.pallas_call(
+        prep_kernel,
+        out_shape=(vmem_out(weight.shape, weight.dtype), part, part, other, other),
+        in_specs=[whole(HBM)] * 4,
+        out_specs=(whole(VMEM),) * 5,
+        scratch_shapes=[SMEM(order.shape, order.dtype), pltpu.SemaphoreType.DMA((6,))],
+        compiler_params=pltpu.CompilerParams(vmem_limit_bytes=16 * 2**20),
+        name="prep",
+        cost_estimate=cost(1 << 26, 16 << 20),
+    )(*in_hbm(order, weight, queries, residual))
 
 
 def attend(q_rows, pieces, biases, diagonal, kv_heads):
@@ -119,69 +184,42 @@
             ref[:, i * cols : (i + 1) * cols] = block.astype(ref.dtype)
 
 
-def side_kernel(late, kv_heads, n_core, order_ref, q_ref, w_ref, *refs):
+def side_kernel(late, kv_heads, n_core, marks_ref, q_ref, w_ref, *refs):
     *piece_refs, away_ref, keep_ref = refs
     rows = away_ref.shape[0]
-    me = lax.axis_index("seq")
-    mine = early_of(order_ref, me)
-    flip = flip_of(order_ref)
-    q_rows = q_ref[half((1 - flip) if late else flip, rows), :]
-    peers = [early_of(order_ref, me ^ p) for p in (1, 2, 3)]
     if late:
-        biases = [None] * 4 + [jnp.where(c > mine, 0.0, FAR) for c in peers]
+        biases = [None] * 4 + [marks_ref[i : i + 1, :] for i in (4, 5, 6)]
     else:
-        biases = [jnp.where(c < mine, 0.0, FAR) for c in peers]
+        biases = [marks_ref[i : i + 1, :] for i in (1, 2, 3)]
     row = lax.broadcasted_iota(jnp.int32, (rows, rows), 0)
     col = lax.broadcasted_iota(jnp.int32, (rows, rows), 1)
-    att = attend(q_rows, [r[...] for r in piece_refs], biases, col <= row, kv_heads)
+    att = attend(q_ref[...], [r[...] for r in piece_refs], biases, col <= row, kv_heads)
     project(att, w_ref, away_ref, keep_ref, n_core)
 
 
-def side(late, kv_heads, n_core, order, queries, weight, pieces):
-    rows, depth = queries.shape[0] // 2, queries.shape[1]
+def side(late, kv_heads, n_core, marks, queries, weight, pieces):
+    rows, depth = queries.shape
     cols = weight.shape[1] // 2
     keys = rows * len(pieces)
     flops = 4 * rows * depth * keys + 2 * rows * depth * weight.shape[1]
     return pl.pallas_call(
         functools.partial(side_kernel, late, kv_heads, n_core),
         out_shape=(
-            jax.ShapeDtypeStruct((rows, cols), jnp.bfloat16),
-            jax.ShapeDtypeStruct((rows, cols), jnp.float32),
+            vmem_out((rows, cols), jnp.bfloat16),
+            vmem_out((rows, cols), jnp.float32),
         ),
-        in_specs=[whole(SMEM)] + [whole(VMEM)] * (2 + len(pieces)),
+        in_specs=[whole(VMEM)] * (3 + len(pieces)),
         out_specs=(whole(VMEM), whole(VMEM)),
         compiler_params=params(),
         name="late_side" if late else "early_side",
         cost_estimate=cost(flops, 16 << 20, rows * depth * keys // HEAD_SIZE),
-    )(order, queries, weight, *pieces)
-
-
-def load_kernel(w_ref, out_ref, sem):
-    copy = pltpu.make_async_copy(w_ref, out_ref, sem)
-    copy.start()
-    copy.wait()
-
-
-def load_weights(weight):
-    return pl.pallas_call(
-        load_kernel,
-        out_shape=vmem_out(weight.shape, weight.dtype),
-        in_specs=[whole(pl.ANY)],
-        out_specs=whole(VMEM),
-        scratch_shapes=[pltpu.SemaphoreType.DMA],
-        compiler_params=pltpu.CompilerParams(vmem_limit_bytes=12 * 2**20),
-        name="load_weights",
-        cost_estimate=cost(1 << 20, 16 << 20),
-    )(weight)
-
-
-def mix_kernel(late, order_ref, res_ref, keep_ref, core_ref, chip_ref, mixed_ref, sq_ref):
-    rows = mixed_ref.shape[0]
-    cols = mixed_ref.shape[1]
-    flip = flip_of(order_ref)
-    res = res_ref[half((1 - flip) if late else flip, rows), :].astype(jnp.float32)
+    )(marks, queries, weight, *pieces)
+
+
+def mix_kernel(res_ref, keep_ref, core_ref, chip_ref, mixed_ref, sq_ref):
+    rows, cols = mixed_ref.shape
     own = keep_ref[:, cols:] + core_ref[:, cols:].astype(jnp.float32)
-    mixed = res + (own + chip_ref[...].astype(jnp.float32))
+    mixed = res_ref[...].astype(jnp.float32) + (own + chip_ref[...].astype(jnp.float32))
     mixed_ref[...] = mixed
     squares = mixed * mixed
     lanes = functools.reduce(
@@ -190,91 +228,117 @@
     sq_ref[...] = jnp.broadcast_to(jnp.sum(lanes.T, axis=0, keepdims=True), sq_ref.shape)
 
 
-def mix(late, order, residual, keep, core, chip):
-    rows, cols = residual.shape[0] // 2, residual.shape[1]
-    return pl.pallas_call(
-        functools.partial(mix_kernel, late),
-        out_shape=(
-            jax.ShapeDtypeStruct((rows, cols), jnp.float32),
-            jax.ShapeDtypeStruct((8, rows), jnp.float32),
-        ),
-        in_specs=[whole(SMEM)] + [whole(VMEM)] * 4,
+def mix(late, residual, keep, core, chip):
+    rows, cols = residual.shape
+    return pl.pallas_call(
+        mix_kernel,
+        out_shape=(vmem_out((rows, cols), jnp.float32), vmem_out((8, rows), jnp.float32)),
+        in_specs=[whole(VMEM)] * 4,
         out_specs=(whole(VMEM), whole(VMEM)),
         compiler_params=params(),
         name="late_mix" if late else "early_mix",
         cost_estimate=cost(1 << 20, 2 << 20),
-    )(order, residual, keep, core, chip)
-
-
-def final_kernel(features, order_ref, gain_ref, early_ref, late_ref, *refs):
-    *sq_refs, out_ref = refs
-    rows, cols = early_ref.shape
-    flip = flip_of(order_ref)
+    )(residual, keep, core, chip)
+
+
+def normed_block(features, mixed_ref, gain, own_ref, other_ref, lanes):
+    rows = mixed_ref.shape[0]
+    totals = own_ref[0:1] + other_ref[0:1]
+    inverse = lax.rsqrt(totals / features + norm_epsilon)
+    inverse = jnp.broadcast_to(inverse, (rows, rows)).T
+    return mixed_ref[:, lanes] * inverse * gain[:, lanes]
+
+
+def norm_kernel(features, gain_ref, mixed_ref, own_ref, other_ref, out_ref):
+    rows, cols = mixed_ref.shape
     gain = gain_ref[...].astype(jnp.float32)
-    totals = functools.reduce(jnp.add, [r[...] for r in sq_refs])
-    for i, (ref, index) in enumerate(((early_ref, flip), (late_ref, 1 - flip))):
-        inverse = lax.rsqrt(totals[8 * i : 8 * i + 1] / features + norm_epsilon)
-        inverse = jnp.broadcast_to(inverse, (rows, rows)).T
-        for j in range(0, cols, rows):
-            block = ref[:, j : j + rows] * inverse * gain[:, j : j + rows]
-            out_ref[half(index, rows), j : j + rows] = block.astype(out_ref.dtype)
-
-
-def final(features, order, gain, early, late, sums):
-    rows, cols = early.shape
-    return pl.pallas_call(
-        functools.partial(final_kernel, features),
-        out_shape=jax.ShapeDtypeStruct((2 * rows, cols), jnp.bfloat16),
-        in_specs=[whole(SMEM)] + [whole(VMEM)] * (3 + len(sums)),
+    for j in range(0, cols, rows):
+        lanes = slice(j, j + rows)
+        block = normed_block(features, mixed_ref, gain, own_ref, other_ref, lanes)
+        out_ref[:, lanes] = block.astype(out_ref.dtype)
+
+
+def early_norm(features, gain, mixed, own, other):
+    return pl.pallas_call(
+        functools.partial(norm_kernel, features),
+        out_shape=vmem_out(mixed.shape, jnp.bfloat16),
+        in_specs=[whole(VMEM)] * 4,
         out_specs=whole(VMEM),
         compiler_params=params(),
-        name="final_norm",
+        name="early_norm",
+        cost_estimate=cost(1 << 20, 1 << 20),
+    )(gain, mixed, own, other)
+
+
+def last_kernel(features, marks_ref, gain_ref, early_ref, mixed_ref, own_ref, other_ref, out_ref):
+    rows, cols = mixed_ref.shape
+    gain = gain_ref[...].astype(jnp.float32)
+    flip = marks_ref[0:1, :] > 0.5
+    for j in range(0, cols, rows):
+        lanes = slice(j, j + rows)
+        late = normed_block(features, mixed_ref, gain, own_ref, other_ref, lanes)
+        early = early_ref[:, lanes].astype(jnp.float32)
+        out_ref[:rows, lanes] = jnp.where(flip, late, early).astype(out_ref.dtype)
+        out_ref[rows:, lanes] = jnp.where(flip, early, late).astype(out_ref.dtype)
+
+
+def late_norm(features, marks, gain, early, mixed, own, other):
+    rows, cols = mixed.shape
+    return pl.pallas_call(
+        functools.partial(last_kernel, features),
+        out_shape=jax.ShapeDtypeStruct((2 * rows, cols), jnp.bfloat16),
+        in_specs=[whole(VMEM)] * 6,
+        out_specs=whole(VMEM),
+        compiler_params=params(),
+        name="late_norm",
         cost_estimate=cost(1 << 20, 2 << 20),
-    )(order, gain.reshape(1, cols), early, late, *sums)
-
-
-def exchange(x, axis, size, step):
-    return lax.ppermute(x, axis, [(i, i ^ step) for i in range(size)])
-
-
-def paired_body(n_seq, n_head, n_core, queries, keys, values, residual, weight, gain, order):
+    )(marks, gain, early, mixed, own, other)
+
+
+def paired_body(n_seq, n_head, n_core, *args):
+    return paired_steps(n_seq, n_head, n_core, *args)
+
+
+def paired_steps(n_seq, n_head, n_core, queries, keys, values, residual, weight, gain, order):
     kv_heads = keys.shape[1] // HEAD_SIZE
     cols = residual.shape[1]
-    early, late = split_halves(order, keys, values)
-    seq = lambda x, step: exchange(x, "seq", n_seq, step)
-    head = lambda x, step: exchange(x, "head", n_head, step)
-
-    early_b = seq(early, 2)
-    early_a = seq(early, 1)
-    late_b = seq(late, 2)
-    early_c = seq(early_b, 1)
-    late_a = seq(late, 1)
-    late_c = seq(late_b, 1)
-    held = load_weights(weight)
-
-    away_e, keep_e = side(
-        False, kv_heads, n_core, order, queries, held, [early_a, early_b, early_c, early]
-    )
-    core_e = head(away_e, 1)
-    chip_e = head((keep_e[:, :cols] + core_e[:, :cols].astype(jnp.float32)).astype(jnp.bfloat16), n_core)
-
-    away_l, keep_l = side(
-        True,
-        kv_heads,
-        n_core,
-        order,
-        queries,
-        held,
-        [early, early_a, early_b, early_c, late_a, late_b, late_c, late],
-    )
-    core_l = head(away_l, 1)
-    chip_l = head((keep_l[:, :cols] + core_l[:, :cols].astype(jnp.float32)).astype(jnp.bfloat16), n_core)
-
-    mixed_e, sq_e = mix(False, order, residual, keep_e, core_e, chip_e)
-    mixed_l, sq_l = mix(True, order, residual, keep_l, core_l, chip_l)
-    own = jnp.concatenate([sq_e, sq_l], axis=0)
-    others = [head(own, step) for step in range(1, n_head)]
-    return final(n_head * cols, order, gain, mixed_e, mixed_l, [own] + others)
+    features = n_head * cols
+
+    def send(x, axis, step):
+        size = n_seq if axis == "seq" else n_head
+        return lax.ppermute(x, axis, [(i, i ^ step) for i in range(size)])
+
+    early, late, marks = split_halves(order, keys, values)
+    early_b = send(early, "seq", 2)
+    early_a = send(early, "seq", 1)
+    late_b = send(late, "seq", 2)
+    early_c = send(early_b, "seq", 1)
+    late_a = send(late, "seq", 1)
+    late_c = send(late_b, "seq", 1)
+    held, q_e, q_l, res_e, res_l = prep(order, weight, queries, residual)
+    row_gain = gain.reshape(1, cols)
+
+    def chip_share(keep, core):
+        return (keep[:, :cols] + core[:, :cols].astype(jnp.float32)).astype(jnp.bfloat16)
+
+    pieces = [early_a, early_b, early_c, early]
+    away_e, keep_e = side(False, kv_heads, n_core, marks, q_e, held, pieces)
+    core_e = send(away_e, "head", 1)
+    chip_e = send(chip_share(keep_e, core_e), "head", n_core)
+
+    pieces = [early, early_a, early_b, early_c, late_a, late_b, late_c, late]
+    away_l, keep_l = side(True, kv_heads, n_core, marks, q_l, held, pieces)
+    core_l = send(away_l, "head", 1)
+    chip_l = send(chip_share(keep_l, core_l), "head", n_core)
+
+    mixed_e, sq_e = mix(False, res_e, keep_e, core_e, chip_e)
+    sum_e = sq_e + send(sq_e, "head", 1)
+    other_e = send(sum_e, "head", n_core)
+    mixed_l, sq_l = mix(True, res_l, keep_l, core_l, chip_l)
+    sum_l = sq_l + send(sq_l, "head", 1)
+    other_l = send(sum_l, "head", n_core)
+    normed_e = early_norm(features, row_gain, mixed_e, sum_e, other_e)
+    return late_norm(features, marks, row_gain, normed_e, mixed_l, sum_l, other_l)
 
 
 def slot_positions(row_ids, block_order, block_rows):

time: 54 us -> 50.6 us (0.937)
  local copies, waits for them, and re-layouts: 6.15 us -> 0.01 us
  Pallas kernels: 10.7 us -> 11.8 us
  starting transfers between devices: 13.9 us -> 15 us
  waiting for transfers between devices: 22.8 us -> 23.4 us
    unnamed x17 -> x2, local copies, waits for them, and re-layouts: 6.14 us -> 0.01 us
    pallas_call x5 -> x6, Pallas kernels: 4.21 us -> 6.43 us  [the longest x1 3.75 us: prep(): pl.pallas_call(prep_kernel, out_shape=(vmem_out(weight.shape, weight.dtyp...]
    ppermute x13 -> x14, starting transfers between devices: 13.9 us -> 15 us  [send(): return lax.ppermute(x, axis, [(i, i ^ step) for i in range(size)])]
    pallas_call x2, Pallas kernels: 6.47 us -> 5.42 us  [side(): pl.pallas_call(functools.partial(side_kernel, late, kv_heads, n_core), ou...]
    ppermute x13 -> x14, waiting for transfers between devices: 22.8 us -> 23.4 us  [send(): return lax.ppermute(x, axis, [(i, i ^ step) for i in range(size)])]
  transfers between devices with their start and end apart: 13 -> 14, of which waited for: 7 -> 8; matrix products, arithmetic and copies ran while one was open for 0% -> 0% of each run, Pallas kernels for 15% -> 19%
where the time goes in v2:
time: 50.6 us; the launch traced here: 50.5 us
  waiting for transfers between devices  23.4 us (46%)
  starting transfers between devices  15 us (30%)
  Pallas kernels  11.8 us (23%)
    ppermute x14, waiting for transfers between devices, send(): return lax.ppermute(x, axis, [(i, i ^ step) for i in range(size)])  23.4 us
    ppermute x14, starting transfers between devices, send(): return lax.ppermute(x, axis, [(i, i ^ step) for i in range(size)])  15 us
    pallas_call x2, Pallas kernels, side(): pl.pallas_call(functools.partial(side_kernel, late, kv_heads, n_core), ou...  5.42 us
    pallas_call x1, Pallas kernels, prep(): pl.pallas_call(prep_kernel, out_shape=(vmem_out(weight.shape, weight.dtyp...  3.75 us
  transfers between devices with their start and end apart: 14, of which 8 were waited for; matrix products, arithmetic and copies ran while one was open for 0% of the time, Pallas kernels for 19%

profile of v2, /device:TPU:0, one launch (start us, length us, event | category | flops | bytes accessed | tf_op | source)
XLA Modules:
  0.0 50.5 jit_solution(6121155378166036078)
XLA Ops:
  0.0 1.0 %split_halves.1 = (bf16[128,512]{1,0:T(8,128)(2,1)S(1)}, bf16[128,512]{1,0:T(8,128)(2,1)S(1)}, f32[8,128]{1,0:T(8,128)S(1)}) custom-call(s32[8]{0:T(128)} %order_hbm.3, bf16[256,256]{1,0:T(8,128)(2,1)} %k_hbm.1, bf16[256,256]{1,0:T(8,128)(2,1)} %v_hbm.1), custom_call_target="tpu_custom_call" | custom-call | flops 1000 | bytes 1048576 | tf_op jit(solution)/shard_map/split_halves/pallas_call | solution.py:87
  1.0 4.1 %collective-permute-start.1 = (bf16[128,512]{1,0:T(8,128)(2,1)S(1)}, bf16[128,512]{1,0:T(8,128)(2,1)S(1)}, u32[]{:S(2)}, u32[]{:S(2)}) collective-permute-start(bf16[128,512]{1,0:T(8,128)(2,1)S(1)} %get-tuple-element.25.refs_3_.refs_0_), channel_id=1, source_target_pairs={{0,8},{4,12},{8,0},{12,4},{1,9},{5,13},{9,1},{13,5},{2,10},{6,14},... | collective-permute-start | bytes 393224 | tf_op jit(solution)/shard_map/ppermute | solution.py:309
  5.1 0.1 collective-permute-start.8
  5.2 1.8 %collective-permute-start = (bf16[128,512]{1,0:T(8,128)(2,1)S(1)}, bf16[128,512]{1,0:T(8,128)(2,1)S(1)}, u32[]{:S(2)}, u32[]{:S(2)}) collective-permute-start(bf16[128,512]{1,0:T(8,128)(2,1)S(1)} %get-tuple-element.25.refs_3_.refs_0_), channel_id=1, source_target_pairs={{0,4},{4,0},{8,12},{12,8},{1,5},{5,1},{9,13},{13,9},{2,6},{6,2},{1... | collective-permute-start | bytes 393224 | tf_op jit(solution)/shard_map/ppermute | solution.py:309
  7.1 8.1 %collective-permute-done.1.refs_1_.refs_2_ = bf16[128,512]{1,0:T(8,128)(2,1)S(1)} collective-permute-done((bf16[128,512]{1,0:T(8,128)(2,1)S(1)}, bf16[128,512]{1,0:T(8,128)(2,1)S(1)}, u32[]{:S(2)}, u32[]{:S(2)}) %collective-permute-start.1) | collective-permute-done | bytes 131104 | tf_op jit(solution)/shard_map/ppermute | solution.py:309
  15.1 0.0 collective-permute-start.2
  15.1 2.0 %collective-permute-start.7 = (bf16[128,512]{1,0:T(8,128)(2,1)S(1)}, bf16[128,512]{1,0:T(8,128)(2,1)S(1)}, u32[]{:S(2)}, u32[]{:S(2)}) collective-permute-start(bf16[128,512]{1,0:T(8,128)(2,1)S(1)} %get-tuple-element.32.refs_7_), channel_id=1, source_target_pairs={{0,4},{4,0},{8,12},{12,8},{1,5},{5,1},{9,13},{13,9},{2,6},{6,2},{1... | collective-permute-start | bytes 393224 | tf_op jit(solution)/shard_map/ppermute | solution.py:309
  17.1 3.8 %prep.1 = (bf16[1024,4096]{1,0:T(8,128)(2,1)S(1)}, bf16[128,1024]{1,0:T(8,128)(2,1)S(1)}, bf16[128,1024]{1,0:T(8,128)(2,1)S(1)}, bf16[128,1024]{1,0:T(8,128)(2,1)S(1)}, bf16[128,1024]{1,0:T(8,128)(2,1)S(1)}) custom-call(s32[8]{0:T(128)} %order_hbm.3, bf16[1024,4096]{1,0:T(8,128)(2,1)} %w_hbm.1, bf16[256,1024]{1,0:T(8,128)(2,1)} %q_hbm.1, bf16[256,1024]{1,0:T(8,128)(2,1)} %r_hbm.1), custom_call_target="tpu_custom_call" | custom-call | flops 67108864 | bytes 16777216 | tf_op jit(solution)/shard_map/prep/pallas_call | solution.py:124
  20.9 0.0 collective-permute-done.8.refs_5_
  20.9 0.1 collective-permute-start.9
  21.0 0.0 collective-permute-done.refs_0_.refs_1_
  21.0 0.3 collective-permute-done.2.refs_2_.refs_3_
  21.3 2.2 %early_side.1 = (bf16[128,2048]{1,0:T(8,128)(2,1)S(1)}, f32[128,2048]{1,0:T(8,128)S(1)}) custom-call(f32[8,128]{1,0:T(8,128)S(1)} %get-tuple-element.21.marks_ref, bf16[128,1024]{1,0:T(8,128)(2,1)S(1)} %get-tuple-element.23.q_ref, bf16[1024,4096]{1,0:T(8,128)(2,1)S(1)} %get-tuple-element.24.w_ref, bf16[128,512]{1,0:T(8,128)(2,1)S(1)} %collective-permute-done.refs_0_.refs_1_, ...), custom_call_target="tpu_custom_call" | custom-call | flops 1342177280 | bytes 16777216 | tf_op jit(solution)/shard_map/early_side/pallas_call | solution.py:205
  23.5 0.0 copy-start
  23.5 0.1 collective-permute-start.3
  23.6 0.4 collective-permute-done.7.refs_4_
  24.0 2.0 %collective-permute-done.9.refs_6_ = bf16[128,512]{1,0:T(8,128)(2,1)S(1)} collective-permute-done((bf16[128,512]{1,0:T(8,128)(2,1)S(1)}, bf16[128,512]{1,0:T(8,128)(2,1)S(1)}, u32[]{:S(2)}, u32[]{:S(2)}) %collective-permute-start.9) | collective-permute-done | bytes 131104 | tf_op jit(solution)/shard_map/ppermute | solution.py:309
  25.9 3.2 %late_side.1 = (bf16[128,2048]{1,0:T(8,128)(2,1)S(1)}, f32[128,2048]{1,0:T(8,128)S(1)}) custom-call(f32[8,128]{1,0:T(8,128)S(1)} %get-tuple-element.21.marks_ref, bf16[128,1024]{1,0:T(8,128)(2,1)S(1)} %get-tuple-element.31.q_ref, bf16[1024,4096]{1,0:T(8,128)(2,1)S(1)} %get-tuple-element.24.w_ref, bf16[128,512]{1,0:T(8,128)(2,1)S(1)} %get-tuple-element.25.refs_3_.refs_0_, ...), custom_call_target="tpu_custom_call" | custom-call | flops 1610612736 | bytes 16777216 | tf_op jit(solution)/shard_map/late_side/pallas_call | solution.py:205
  29.1 0.1 collective-permute-start.10
  29.2 0.0 collective-permute-done.3.core_ref
  29.2 0.1 add_convert_fusion.1
  29.3 1.9 %collective-permute-start.4 = (bf16[128,1024]{1,0:T(8,128)(2,1)S(1)}, bf16[128,1024]{1,0:T(8,128)(2,1)S(1)}, u32[]{:S(2)}, u32[]{:S(2)}) collective-permute-start(bf16[128,1024]{1,0:T(8,128)(2,1)S(1)} %add_convert_fusion.1), channel_id=1, source_target_pairs={{0,2},{1,3},{2,0},{3,1},{4,6},{5,7},{6,4},{7,5},{8,10},{9,11},{10,... | collective-permute-start | bytes 786440 | tf_op jit(solution)/shard_map/ppermute | solution.py:309
  31.1 0.0 collective-permute-done.10.core_ref
  31.1 0.1 add_convert_fusion
  31.2 1.8 %collective-permute-start.11 = (bf16[128,1024]{1,0:T(8,128)(2,1)S(1)}, bf16[128,1024]{1,0:T(8,128)(2,1)S(1)}, u32[]{:S(2)}, u32[]{:S(2)}) collective-permute-start(bf16[128,1024]{1,0:T(8,128)(2,1)S(1)} %add_convert_fusion), channel_id=1, source_target_pairs={{0,2},{1,3},{2,0},{3,1},{4,6},{5,7},{6,4},{7,5},{8,10},{9,11},{10,... | collective-permute-start | bytes 786440 | tf_op jit(solution)/shard_map/ppermute | solution.py:309
  33.0 5.5 %collective-permute-done.4.chip_ref = bf16[128,1024]{1,0:T(8,128)(2,1)S(1)} collective-permute-done((bf16[128,1024]{1,0:T(8,128)(2,1)S(1)}, bf16[128,1024]{1,0:T(8,128)(2,1)S(1)}, u32[]{:S(2)}, u32[]{:S(2)}) %collective-permute-start.4) | collective-permute-done | bytes 262176 | tf_op jit(solution)/shard_map/ppermute | solution.py:309
  38.5 0.2 early_mix.1
  38.8 0.1 collective-permute-start.5
  38.8 4.9 %collective-permute-done.11.chip_ref = bf16[128,1024]{1,0:T(8,128)(2,1)S(1)} collective-permute-done((bf16[128,1024]{1,0:T(8,128)(2,1)S(1)}, bf16[128,1024]{1,0:T(8,128)(2,1)S(1)}, u32[]{:S(2)}, u32[]{:S(2)}) %collective-permute-start.11) | collective-permute-done | bytes 262176 | tf_op jit(solution)/shard_map/ppermute | solution.py:309
  43.7 0.2 late_mix.1
  43.9 0.1 collective-permute-start.12
  44.0 0.0 collective-permute-done.5
  44.0 1.8 %collective-permute-start.6 = (f32[8,128]{1,0:T(8,128)S(1)}, f32[8,128]{1,0:T(8,128)S(1)}, u32[]{:S(2)}, u32[]{:S(2)}) collective-permute-start(f32[8,128]{1,0:T(8,128)S(1)} %add.13.own_ref), channel_id=1, source_target_pairs={{0,2},{1,3},{2,0},{3,1},{4,6},{5,7},{6,4},{7,5},{8,10},{9,11},{10,... | collective-permute-start | bytes 12296 | tf_op jit(solution)/shard_map/ppermute | solution.py:309
  45.8 0.0 collective-permute-done.12
  45.9 1.1 %collective-permute-start.13 = (f32[8,128]{1,0:T(8,128)S(1)}, f32[8,128]{1,0:T(8,128)S(1)}, u32[]{:S(2)}, u32[]{:S(2)}) collective-permute-start(f32[8,128]{1,0:T(8,128)S(1)} %add.15.own_ref), channel_id=1, source_target_pairs={{0,2},{1,3},{2,0},{3,1},{4,6},{5,7},{6,4},{7,5},{8,10},{9,11},{10,... | collective-permute-start | bytes 12296 | tf_op jit(solution)/shard_map/ppermute | solution.py:309
  46.9 0.0 copy-done
  46.9 0.8 %collective-permute-done.6.other_ref = f32[8,128]{1,0:T(8,128)S(1)} collective-permute-done((f32[8,128]{1,0:T(8,128)S(1)}, f32[8,128]{1,0:T(8,128)S(1)}, u32[]{:S(2)}, u32[]{:S(2)}) %collective-permute-start.6) | collective-permute-done | bytes 4128 | tf_op jit(solution)/shard_map/ppermute | solution.py:309
  47.7 0.2 early_norm.1.early_ref
  47.9 1.5 %collective-permute-done.13.other_ref = f32[8,128]{1,0:T(8,128)S(1)} collective-permute-done((f32[8,128]{1,0:T(8,128)S(1)}, f32[8,128]{1,0:T(8,128)S(1)}, u32[]{:S(2)}, u32[]{:S(2)}) %collective-permute-start.13) | collective-permute-done | bytes 4128 | tf_op jit(solution)/shard_map/ppermute | solution.py:309
  49.5 1.0 %late_norm.1 = bf16[256,1024]{1,0:T(8,128)(2,1)} custom-call(f32[8,128]{1,0:T(8,128)S(1)} %get-tuple-element.21.marks_ref, bf16[1,1024]{1,0:T(2,128)(2,1)S(1)} %reshape.3.gain_ref, bf16[128,1024]{1,0:T(8,128)(2,1)S(1)} %early_norm.1.early_ref, f32[128,1024]{1,0:T(8,128)S(1)} %get-tuple-element.35.mixed_ref, f32[8,128]{1,0:T(8,128)S(1)} %add.15.own_ref, ...), custom_call_target="tpu_custom_call" | custom-call | flops 1048576 | bytes 2097152 | tf_op jit(solution)/shard_map/late_norm/pallas_call | solution.py:287
  (3 shorter events, 0.0 us)
Async XLA Ops:
  1.0 14.1 %collective-permute-start.1 = (bf16[128,512]{1,0:T(8,128)(2,1)S(1)}, bf16[128,512]{1,0:T(8,128)(2,1)S(1)}, u32[]{:S(2)}, u32[]{:S(2)}) collective-permute-start(bf16[128,512]{1,0:T(8,128)(2,1)S(1)} %get-tuple-element.25.refs_3_.refs_0_), channel_id=1, source_target_pairs={{0,8},{4,12},{8,0},{12,4},{1,9},{5,13},{9,1},{13,5},{2,10},{6,14},... | collective-permute-start | bytes 393224 | tf_op jit(solution)/shard_map/ppermute | solution.py:309
  5.1 15.8 %collective-permute-start.8 = (bf16[128,512]{1,0:T(8,128)(2,1)S(1)}, bf16[128,512]{1,0:T(8,128)(2,1)S(1)}, u32[]{:S(2)}, u32[]{:S(2)}) collective-permute-start(bf16[128,512]{1,0:T(8,128)(2,1)S(1)} %get-tuple-element.32.refs_7_), channel_id=1, source_target_pairs={{0,8},{4,12},{8,0},{12,4},{1,9},{5,13},{9,1},{13,5},{2,10},{6,14},... | collective-permute-start | bytes 393224 | tf_op jit(solution)/shard_map/ppermute | solution.py:309
  5.2 15.8 %collective-permute-start = (bf16[128,512]{1,0:T(8,128)(2,1)S(1)}, bf16[128,512]{1,0:T(8,128)(2,1)S(1)}, u32[]{:S(2)}, u32[]{:S(2)}) collective-permute-start(bf16[128,512]{1,0:T(8,128)(2,1)S(1)} %get-tuple-element.25.refs_3_.refs_0_), channel_id=1, source_target_pairs={{0,4},{4,0},{8,12},{12,8},{1,5},{5,1},{9,13},{13,9},{2,6},{6,2},{1... | collective-permute-start | bytes 393224 | tf_op jit(solution)/shard_map/ppermute | solution.py:309
  15.1 6.2 %collective-permute-start.2 = (bf16[128,512]{1,0:T(8,128)(2,1)S(1)}, bf16[128,512]{1,0:T(8,128)(2,1)S(1)}, u32[]{:S(2)}, u32[]{:S(2)}) collective-permute-start(bf16[128,512]{1,0:T(8,128)(2,1)S(1)} %collective-permute-done.1.refs_1_.refs_2_), channel_id=1, source_target_pairs={{0,4},{4,0},{8,12},{12,8},{1,5},{5,1},{9,13},{13,9},{2,6},{6,2},{1... | collective-permute-start | bytes 393224 | tf_op jit(solution)/shard_map/ppermute | solution.py:309
  15.1 8.9 %collective-permute-start.7 = (bf16[128,512]{1,0:T(8,128)(2,1)S(1)}, bf16[128,512]{1,0:T(8,128)(2,1)S(1)}, u32[]{:S(2)}, u32[]{:S(2)}) collective-permute-start(bf16[128,512]{1,0:T(8,128)(2,1)S(1)} %get-tuple-element.32.refs_7_), channel_id=1, source_target_pairs={{0,4},{4,0},{8,12},{12,8},{1,5},{5,1},{9,13},{13,9},{2,6},{6,2},{1... | collective-permute-start | bytes 393224 | tf_op jit(solution)/shard_map/ppermute | solution.py:309
  20.9 5.0 %collective-permute-start.9 = (bf16[128,512]{1,0:T(8,128)(2,1)S(1)}, bf16[128,512]{1,0:T(8,128)(2,1)S(1)}, u32[]{:S(2)}, u32[]{:S(2)}) collective-permute-start(bf16[128,512]{1,0:T(8,128)(2,1)S(1)} %collective-permute-done.8.refs_5_), channel_id=1, source_target_pairs={{0,4},{4,0},{8,12},{12,8},{1,5},{5,1},{9,13},{13,9},{2,6},{6,2},{1... | collective-permute-start | bytes 393224 | tf_op jit(solution)/shard_map/ppermute | solution.py:309
  23.5 23.4 %copy-start = (bf16[1024]{0:T(1024)(128)(2,1)S(1)}, bf16[1024]{0:T(1024)(128)(2,1)}, u32[]{:S(2)}) copy-start(bf16[1024]{0:T(1024)(128)(2,1)} %param.12) | copy-start | bytes 6148
  23.5 5.7 %collective-permute-start.3 = (bf16[128,2048]{1,0:T(8,128)(2,1)S(1)}, bf16[128,2048]{1,0:T(8,128)(2,1)S(1)}, u32[]{:S(2)}, u32[]{:S(2)}) collective-permute-start(bf16[128,2048]{1,0:T(8,128)(2,1)S(1)} %get-tuple-element.27), channel_id=1, source_target_pairs={{0,1},{1,0},{2,3},{3,2},{4,5},{5,4},{6,7},{7,6},{8,9},{9,8},{10,11... | collective-permute-start | bytes 1572872 | tf_op jit(solution)/shard_map/ppermute | solution.py:309
  29.1 2.0 %collective-permute-start.10 = (bf16[128,2048]{1,0:T(8,128)(2,1)S(1)}, bf16[128,2048]{1,0:T(8,128)(2,1)S(1)}, u32[]{:S(2)}, u32[]{:S(2)}) collective-permute-start(bf16[128,2048]{1,0:T(8,128)(2,1)S(1)} %get-tuple-element.34), channel_id=1, source_target_pairs={{0,1},{1,0},{2,3},{3,2},{4,5},{5,4},{6,7},{7,6},{8,9},{9,8},{10,11... | collective-permute-start | bytes 1572872 | tf_op jit(solution)/shard_map/ppermute | solution.py:309
  29.3 9.2 %collective-permute-start.4 = (bf16[128,1024]{1,0:T(8,128)(2,1)S(1)}, bf16[128,1024]{1,0:T(8,128)(2,1)S(1)}, u32[]{:S(2)}, u32[]{:S(2)}) collective-permute-start(bf16[128,1024]{1,0:T(8,128)(2,1)S(1)} %add_convert_fusion.1), channel_id=1, source_target_pairs={{0,2},{1,3},{2,0},{3,1},{4,6},{5,7},{6,4},{7,5},{8,10},{9,11},{10,... | collective-permute-start | bytes 786440 | tf_op jit(solution)/shard_map/ppermute | solution.py:309
  31.2 12.5 %collective-permute-start.11 = (bf16[128,1024]{1,0:T(8,128)(2,1)S(1)}, bf16[128,1024]{1,0:T(8,128)(2,1)S(1)}, u32[]{:S(2)}, u32[]{:S(2)}) collective-permute-start(bf16[128,1024]{1,0:T(8,128)(2,1)S(1)} %add_convert_fusion), channel_id=1, source_target_pairs={{0,2},{1,3},{2,0},{3,1},{4,6},{5,7},{6,4},{7,5},{8,10},{9,11},{10,... | collective-permute-start | bytes 786440 | tf_op jit(solution)/shard_map/ppermute | solution.py:309
  38.8 5.3 %collective-permute-start.5 = (f32[8,128]{1,0:T(8,128)S(1)}, f32[8,128]{1,0:T(8,128)S(1)}, u32[]{:S(2)}, u32[]{:S(2)}) collective-permute-start(f32[8,128]{1,0:T(8,128)S(1)} %get-tuple-element.29), channel_id=1, source_target_pairs={{0,1},{1,0},{2,3},{3,2},{4,5},{5,4},{6,7},{7,6},{8,9},{9,8},{10,11... | collective-permute-start | bytes 12296 | tf_op jit(solution)/shard_map/ppermute | solution.py:309
  43.9 1.9 %collective-permute-start.12 = (f32[8,128]{1,0:T(8,128)S(1)}, f32[8,128]{1,0:T(8,128)S(1)}, u32[]{:S(2)}, u32[]{:S(2)}) collective-permute-start(f32[8,128]{1,0:T(8,128)S(1)} %get-tuple-element.36), channel_id=1, source_target_pairs={{0,1},{1,0},{2,3},{3,2},{4,5},{5,4},{6,7},{7,6},{8,9},{9,8},{10,11... | collective-permute-start | bytes 12296 | tf_op jit(solution)/shard_map/ppermute | solution.py:309
  44.0 3.7 %collective-permute-start.6 = (f32[8,128]{1,0:T(8,128)S(1)}, f32[8,128]{1,0:T(8,128)S(1)}, u32[]{:S(2)}, u32[]{:S(2)}) collective-permute-start(f32[8,128]{1,0:T(8,128)S(1)} %add.13.own_ref), channel_id=1, source_target_pairs={{0,2},{1,3},{2,0},{3,1},{4,6},{5,7},{6,4},{7,5},{8,10},{9,11},{10,... | collective-permute-start | bytes 12296 | tf_op jit(solution)/shard_map/ppermute | solution.py:309
  45.9 3.6 %collective-permute-start.13 = (f32[8,128]{1,0:T(8,128)S(1)}, f32[8,128]{1,0:T(8,128)S(1)}, u32[]{:S(2)}, u32[]{:S(2)}) collective-permute-start(f32[8,128]{1,0:T(8,128)S(1)} %add.15.own_ref), channel_id=1, source_target_pairs={{0,2},{1,3},{2,0},{3,1},{4,6},{5,7},{6,4},{7,5},{8,10},{9,11},{10,... | collective-permute-start | bytes 12296 | tf_op jit(solution)/shard_map/ppermute | solution.py:309

commit v3 on v2

--- a/solution.py
+++ b/solution.py
@@ -133,92 +133,192 @@
     )(*in_hbm(order, weight, queries, residual))
 
 
-def attend(q_rows, pieces, biases, diagonal, kv_heads):
-    rows = q_rows.shape[0]
+FACTOR = HEAD_SIZE ** (-0.5) * math.log2(math.e)
+
+
+def head_views(q_rows, pieces, kv_heads):
     width = kv_heads * HEAD_SIZE
     group = q_rows.shape[1] // width
-    factor = HEAD_SIZE ** (-0.5) * math.log2(math.e)
-    outs = []
     for h in range(kv_heads):
         lanes = slice(h * HEAD_SIZE, (h + 1) * HEAD_SIZE)
         v_lanes = slice(width + h * HEAD_SIZE, width + (h + 1) * HEAD_SIZE)
         keys = jnp.concatenate([p[:, lanes] for p in pieces], axis=0)
         vals = jnp.concatenate([p[:, v_lanes] for p in pieces], axis=0)
-        heads = [
-            q_rows[:, (h * group + g) * HEAD_SIZE : (h * group + g + 1) * HEAD_SIZE]
-            for g in range(group)
-        ]
-        stacked = jnp.concatenate(heads, axis=0)
-        scores = lax.dot_general(
-            stacked, keys, (((1,), (1,)), ((), ())), preferred_element_type=jnp.float32
-        )
-        parts = []
-        for j, bias in enumerate(biases):
-            part = scores[:, j * rows : (j + 1) * rows]
-            if bias is not None:
-                part = part + bias
-            parts.append(part)
-        last = scores[:, len(biases) * rows :].reshape(group, rows, rows)
-        parts.append(jnp.where(diagonal[None], last, FAR).reshape(group * rows, rows))
-        peak = functools.reduce(jnp.maximum, parts)
-        peak = jnp.max(peak, axis=1, keepdims=True)
-        weights = [jnp.exp2((part - peak) * factor) for part in parts]
-        total = jnp.sum(functools.reduce(jnp.add, weights), axis=1, keepdims=True)
-        rounded = jnp.concatenate([w.astype(jnp.bfloat16) for w in weights], axis=1)
-        mixed = lax.dot_general(
-            rounded, vals, (((1,), (0,)), ((), ())), preferred_element_type=jnp.float32
-        )
-        mixed = (mixed / total).astype(jnp.bfloat16)
-        outs += [mixed[g * rows : (g + 1) * rows] for g in range(group)]
-    return jnp.concatenate(outs, axis=1)
-
-
-def project(att, w_ref, away_ref, keep_ref, n_core):
+        firsts = [(h * group + g) * HEAD_SIZE for g in range(group)]
+        stacked = jnp.concatenate([q_rows[:, f : f + HEAD_SIZE] for f in firsts], axis=0)
+        yield stacked, keys, vals
+
+
+def softmax_terms(stacked, keys, biases, diagonal):
+    scores = lax.dot_general(
+        stacked, keys, (((1,), (1,)), ((), ())), preferred_element_type=jnp.float32
+    )
+    rows = keys.shape[0] // (len(biases) + (diagonal is not None))
+    parts = []
+    for j, bias in enumerate(biases):
+        part = scores[:, j * rows : (j + 1) * rows]
+        parts.append(part if bias is None else part + bias)
+    if diagonal is not None:
+        last = scores[:, len(biases) * rows :].reshape(-1, rows, rows)
+        parts.append(jnp.where(diagonal[None], last, FAR).reshape(-1, rows))
+    peak = jnp.max(functools.reduce(jnp.maximum, parts), axis=1, keepdims=True)
+    return parts, peak
+
+
+def weigh(parts, peak, vals):
+    weights = [jnp.exp2((part - peak) * FACTOR) for part in parts]
+    total = jnp.sum(functools.reduce(jnp.add, weights), axis=1, keepdims=True)
+    rounded = jnp.concatenate([w.astype(jnp.bfloat16) for w in weights], axis=1)
+    mixed = lax.dot_general(
+        rounded, vals, (((1,), (0,)), ((), ())), preferred_element_type=jnp.float32
+    )
+    return total, mixed
+
+
+def unstack(mixed, rows):
+    return [mixed[i : i + rows] for i in range(0, mixed.shape[0], rows)]
+
+
+def lower(rows):
+    row = lax.broadcasted_iota(jnp.int32, (rows, rows), 0)
+    col = lax.broadcasted_iota(jnp.int32, (rows, rows), 1)
+    return col <= row
+
+
+def first_columns(att, w_ref, away_ref, n_core):
     head = lax.axis_index("head")
     chip, core = head // n_core, head % n_core
-    cols = away_ref.shape[1] // 2
-    for i, owner_chip in enumerate((1 - chip, chip)):
-        for ref, owner_core in ((away_ref, 1 - core), (keep_ref, core)):
-            start = pl.multiple_of((owner_chip * n_core + owner_core) * cols, cols)
-            block = jnp.dot(att, w_ref[:, pl.ds(start, cols)], preferred_element_type=jnp.float32)
-            ref[:, i * cols : (i + 1) * cols] = block.astype(ref.dtype)
-
-
-def side_kernel(late, kv_heads, n_core, marks_ref, q_ref, w_ref, *refs):
-    *piece_refs, away_ref, keep_ref = refs
+    cols = away_ref.shape[1]
+    start = pl.multiple_of(((1 - chip) * n_core + 1 - core) * cols, cols)
+    block = jnp.dot(att, w_ref[:, pl.ds(start, cols)], preferred_element_type=jnp.float32)
+    away_ref[...] = block.astype(away_ref.dtype)
+
+
+def early_kernel(kv_heads, n_core, marks_ref, q_ref, w_ref, *refs):
+    *piece_refs, att_ref, away_ref = refs
     rows = away_ref.shape[0]
-    if late:
-        biases = [None] * 4 + [marks_ref[i : i + 1, :] for i in (4, 5, 6)]
-    else:
-        biases = [marks_ref[i : i + 1, :] for i in (1, 2, 3)]
-    row = lax.broadcasted_iota(jnp.int32, (rows, rows), 0)
-    col = lax.broadcasted_iota(jnp.int32, (rows, rows), 1)
-    att = attend(q_ref[...], [r[...] for r in piece_refs], biases, col <= row, kv_heads)
-    project(att, w_ref, away_ref, keep_ref, n_core)
-
-
-def side(late, kv_heads, n_core, marks, queries, weight, pieces):
+    biases = [marks_ref[i : i + 1, :] for i in (1, 2, 3)]
+    outs = []
+    for stacked, keys, vals in head_views(q_ref[...], [r[...] for r in piece_refs], kv_heads):
+        parts, peak = softmax_terms(stacked, keys, biases, lower(rows))
+        total, mixed = weigh(parts, peak, vals)
+        outs += unstack((mixed / total).astype(jnp.bfloat16), rows)
+    att = jnp.concatenate(outs, axis=1)
+    att_ref[...] = att
+    first_columns(att, w_ref, away_ref, n_core)
+
+
+def ahead_kernel(kv_heads, q_ref, *refs):
+    *piece_refs, peak_ref, total_ref, mixed_ref = refs
+    rows = q_ref.shape[0]
+    views = head_views(q_ref[...], [r[...] for r in piece_refs], kv_heads)
+    for h, (stacked, keys, vals) in enumerate(views):
+        parts, peak = softmax_terms(stacked, keys, [None] * 4, lower(rows))
+        total, mixed = weigh(parts, peak, vals)
+        peak_ref[h] = jnp.broadcast_to(peak, mixed.shape)
+        total_ref[h] = jnp.broadcast_to(total, mixed.shape)
+        mixed_ref[h] = mixed
+
+
+def late_kernel(kv_heads, n_core, marks_ref, q_ref, w_ref, peak_ref, total_ref, mixed_ref, *refs):
+    *piece_refs, att_ref, away_ref = refs
+    rows = away_ref.shape[0]
+    biases = [marks_ref[i : i + 1, :] for i in (4, 5, 6)]
+    outs = []
+    views = head_views(q_ref[...], [r[...] for r in piece_refs], kv_heads)
+    for h, (stacked, keys, vals) in enumerate(views):
+        parts, peak = softmax_terms(stacked, keys, biases, None)
+        before = peak_ref[h]
+        peak = jnp.maximum(peak, before)
+        factor = jnp.exp2((before - peak) * FACTOR)
+        total, mixed = weigh(parts, peak, vals)
+        total = total + total_ref[h] * factor
+        mixed = mixed + mixed_ref[h] * factor
+        outs += unstack((mixed / total).astype(jnp.bfloat16), rows)
+    att = jnp.concatenate(outs, axis=1)
+    att_ref[...] = att
+    first_columns(att, w_ref, away_ref, n_core)
+
+
+def attend_early(kv_heads, n_core, marks, queries, weight, pieces):
     rows, depth = queries.shape
-    cols = weight.shape[1] // 2
+    cols = weight.shape[1] // (2 * n_core)
     keys = rows * len(pieces)
-    flops = 4 * rows * depth * keys + 2 * rows * depth * weight.shape[1]
-    return pl.pallas_call(
-        functools.partial(side_kernel, late, kv_heads, n_core),
+    return pl.pallas_call(
+        functools.partial(early_kernel, kv_heads, n_core),
+        out_shape=(vmem_out(queries.shape, jnp.bfloat16), vmem_out((rows, cols), jnp.bfloat16)),
+        in_specs=[whole(VMEM)] * (3 + len(pieces)),
+        out_specs=(whole(VMEM),) * 2,
+        compiler_params=params(),
+        name="attend_early",
+        cost_estimate=cost(4 * rows * depth * keys + 2 * rows * depth * cols, 4 << 20, 1 << 20),
+    )(marks, queries, weight, *pieces)
+
+
+def attend_ahead(kv_heads, queries, pieces):
+    rows, depth = queries.shape
+    keys = rows * len(pieces)
+    state = vmem_out((kv_heads, rows * depth // (kv_heads * HEAD_SIZE), HEAD_SIZE), jnp.float32)
+    return pl.pallas_call(
+        functools.partial(ahead_kernel, kv_heads),
+        out_shape=(state,) * 3,
+        in_specs=[whole(VMEM)] * (1 + len(pieces)),
+        out_specs=(whole(VMEM),) * 3,
+        compiler_params=params(),
+        name="attend_ahead",
+        cost_estimate=cost(4 * rows * depth * keys, 4 << 20, 1 << 20),
+    )(queries, *pieces)
+
+
+def attend_late(kv_heads, n_core, marks, queries, weight, state, pieces):
+    rows, depth = queries.shape
+    cols = weight.shape[1] // (2 * n_core)
+    keys = rows * len(pieces)
+    return pl.pallas_call(
+        functools.partial(late_kernel, kv_heads, n_core),
+        out_shape=(vmem_out(queries.shape, jnp.bfloat16), vmem_out((rows, cols), jnp.bfloat16)),
+        in_specs=[whole(VMEM)] * (6 + len(pieces)),
+        out_specs=(whole(VMEM),) * 2,
+        compiler_params=params(),
+        name="attend_late",
+        cost_estimate=cost(4 * rows * depth * keys + 2 * rows * depth * cols, 4 << 20, 1 << 20),
+    )(marks, queries, weight, *state, *pieces)
+
+
+def rest_kernel(n_core, att_ref, w_ref, share_ref, away_ref, keep_ref):
+    head = lax.axis_index("head")
+    chip, core = head // n_core, head % n_core
+    cols = keep_ref.shape[1]
+    owners = ((1 - chip, core, share_ref), (chip, 1 - core, away_ref), (chip, core, keep_ref))
+    for owner_chip, owner_core, ref in owners:
+        start = pl.multiple_of((owner_chip * n_core + owner_core) * cols, cols)
+        block = jnp.dot(
+            att_ref[...], w_ref[:, pl.ds(start, cols)], preferred_element_type=jnp.float32
+        )
+        ref[...] = block.astype(ref.dtype)
+
+
+def project_rest(late, n_core, att, weight):
+    rows, depth = att.shape
+    cols = weight.shape[1] // (2 * n_core)
+    return pl.pallas_call(
+        functools.partial(rest_kernel, n_core),
         out_shape=(
+            vmem_out((rows, cols), jnp.float32),
             vmem_out((rows, cols), jnp.bfloat16),
             vmem_out((rows, cols), jnp.float32),
         ),
-        in_specs=[whole(VMEM)] * (3 + len(pieces)),
-        out_specs=(whole(VMEM), whole(VMEM)),
-        compiler_params=params(),
-        name="late_side" if late else "early_side",
-        cost_estimate=cost(flops, 16 << 20, rows * depth * keys // HEAD_SIZE),
-    )(marks, queries, weight, *pieces)
+        in_specs=[whole(VMEM)] * 2,
+        out_specs=(whole(VMEM),) * 3,
+        compiler_params=params(),
+        name="late_rest" if late else "early_rest",
+        cost_estimate=cost(6 * rows * depth * cols, 8 << 20),
+    )(att, weight)
 
 
 def mix_kernel(res_ref, keep_ref, core_ref, chip_ref, mixed_ref, sq_ref):
     rows, cols = mixed_ref.shape
-    own = keep_ref[:, cols:] + core_ref[:, cols:].astype(jnp.float32)
+    own = keep_ref[...] + core_ref[...].astype(jnp.float32)
     mixed = res_ref[...].astype(jnp.float32) + (own + chip_ref[...].astype(jnp.float32))
     mixed_ref[...] = mixed
     squares = mixed * mixed
@@ -318,18 +418,23 @@
     held, q_e, q_l, res_e, res_l = prep(order, weight, queries, residual)
     row_gain = gain.reshape(1, cols)
 
-    def chip_share(keep, core):
-        return (keep[:, :cols] + core[:, :cols].astype(jnp.float32)).astype(jnp.bfloat16)
+    def project(att, away, late):
+        core = send(away, "head", 1)
+        share, away, keep = project_rest(late, n_core, att, held)
+        summed = (share + core.astype(jnp.float32)).astype(jnp.bfloat16)
+        chip = send(summed, "head", n_core)
+        core = send(away, "head", 1)
+        return keep, core, chip
 
     pieces = [early_a, early_b, early_c, early]
-    away_e, keep_e = side(False, kv_heads, n_core, marks, q_e, held, pieces)
-    core_e = send(away_e, "head", 1)
-    chip_e = send(chip_share(keep_e, core_e), "head", n_core)
-
-    pieces = [early, early_a, early_b, early_c, late_a, late_b, late_c, late]
-    away_l, keep_l = side(True, kv_heads, n_core, marks, q_l, held, pieces)
-    core_l = send(away_l, "head", 1)
-    chip_l = send(chip_share(keep_l, core_l), "head", n_core)
+    att, away = attend_early(kv_heads, n_core, marks, q_e, held, pieces)
+    keep_e, core_e, chip_e = project(att, away, False)
+
+    pieces = [early, early_a, early_b, early_c, late]
+    state = attend_ahead(kv_heads, q_l, pieces)
+    pieces = [late_a, late_b, late_c]
+    att, away = attend_late(kv_heads, n_core, marks, q_l, held, state, pieces)
+    keep_l, core_l, chip_l = project(att, away, True)
 
     mixed_e, sq_e = mix(False, res_e, keep_e, core_e, chip_e)
     sum_e = sq_e + send(sq_e, "head", 1)

time: 50.6 us -> 53.2 us (1.051)
  starting transfers between devices: 15 us -> 16.6 us
  Pallas kernels: 11.8 us -> 12.7 us
    ppermute x14 -> x16, starting transfers between devices: 15 us -> 16.6 us  [send(): return lax.ppermute(x, axis, [(i, i ^ step) for i in range(size)])]
    pallas_call x2 -> x5, Pallas kernels: 5.42 us -> 6.29 us  [the longest x2 2.04 us: project_rest(): pl.pallas_call(functools.partial(rest_kernel, n_core), out_shape=(vmem_ou...]
    ppermute x14 -> x16, waiting for transfers between devices: 23.4 us -> 23.4 us  [send(): return lax.ppermute(x, axis, [(i, i ^ step) for i in range(size)])]
  transfers between devices with their start and end apart: 14 -> 16, of which waited for: 8 -> 8; matrix products, arithmetic and copies ran while one was open for 0% -> 0% of each run, Pallas kernels for 19% -> 20%
where the time goes in v3:
time: 53.2 us; the launch traced here: 53 us
  waiting for transfers between devices  23.4 us (44%)
  starting transfers between devices  16.6 us (31%)
  Pallas kernels  12.7 us (24%)
    ppermute x16, waiting for transfers between devices, send(): return lax.ppermute(x, axis, [(i, i ^ step) for i in range(size)])  23.4 us
    ppermute x16, starting transfers between devices, send(): return lax.ppermute(x, axis, [(i, i ^ step) for i in range(size)])  16.6 us
    pallas_call x1, Pallas kernels, prep(): pl.pallas_call(prep_kernel, out_shape=(vmem_out(weight.shape, weight.dtyp...  3.75 us
    pallas_call x2, Pallas kernels, project_rest(): pl.pallas_call(functools.partial(rest_kernel, n_core), out_shape=(vmem_ou...  2.04 us
    pallas_call x1, Pallas kernels, attend_ahead(): pl.pallas_call(functools.partial(ahead_kernel, kv_heads), out_shape=(stat...  1.52 us
    pallas_call x1, Pallas kernels, attend_early(): pl.pallas_call(functools.partial(early_kernel, kv_heads, n_core), out_sha...  1.41 us
    pallas_call x1, Pallas kernels, attend_late(): pl.pallas_call(functools.partial(late_kernel, kv_heads, n_core), out_shap...  1.32 us
  transfers between devices with their start and end apart: 16, of which 8 were waited for; matrix products, arithmetic and copies ran while one was open for 0% of the time, Pallas kernels for 20%

profile of v3, /device:TPU:0, one launch (start us, length us, event | category | flops | bytes accessed | tf_op | source)
XLA Modules:
  0.0 53.0 jit_solution(12712494384521212480)
XLA Ops:
  0.0 1.0 %split_halves.1 = (bf16[128,512]{1,0:T(8,128)(2,1)S(1)}, bf16[128,512]{1,0:T(8,128)(2,1)S(1)}, f32[8,128]{1,0:T(8,128)S(1)}) custom-call(s32[8]{0:T(128)} %order_hbm.3, bf16[256,256]{1,0:T(8,128)(2,1)} %k_hbm.1, bf16[256,256]{1,0:T(8,128)(2,1)} %v_hbm.1), custom_call_target="tpu_custom_call" | custom-call | flops 1000 | bytes 1048576 | tf_op jit(solution)/shard_map/split_halves/pallas_call | solution.py:87
  1.0 4.1 %collective-permute-start.1 = (bf16[128,512]{1,0:T(8,128)(2,1)S(1)}, bf16[128,512]{1,0:T(8,128)(2,1)S(1)}, u32[]{:S(2)}, u32[]{:S(2)}) collective-permute-start(bf16[128,512]{1,0:T(8,128)(2,1)S(1)} %get-tuple-element.34.refs_3_.refs_0_), channel_id=1, source_target_pairs={{0,8},{4,12},{8,0},{12,4},{1,9},{5,13},{9,1},{13,5},{2,10},{6,14},... | collective-permute-start | bytes 393224 | tf_op jit(solution)/shard_map/ppermute | solution.py:409
  5.1 1.6 %collective-permute-start = (bf16[128,512]{1,0:T(8,128)(2,1)S(1)}, bf16[128,512]{1,0:T(8,128)(2,1)S(1)}, u32[]{:S(2)}, u32[]{:S(2)}) collective-permute-start(bf16[128,512]{1,0:T(8,128)(2,1)S(1)} %get-tuple-element.34.refs_3_.refs_0_), channel_id=1, source_target_pairs={{0,4},{4,0},{8,12},{12,8},{1,5},{5,1},{9,13},{13,9},{2,6},{6,2},{1... | collective-permute-start | bytes 393224 | tf_op jit(solution)/shard_map/ppermute | solution.py:409
  6.7 4.8 %collective-permute-done.1.refs_1_.refs_2_ = bf16[128,512]{1,0:T(8,128)(2,1)S(1)} collective-permute-done((bf16[128,512]{1,0:T(8,128)(2,1)S(1)}, bf16[128,512]{1,0:T(8,128)(2,1)S(1)}, u32[]{:S(2)}, u32[]{:S(2)}) %collective-permute-start.1) | collective-permute-done | bytes 131104 | tf_op jit(solution)/shard_map/ppermute | solution.py:409
  11.5 0.6 %collective-permute-start.2 = (bf16[128,512]{1,0:T(8,128)(2,1)S(1)}, bf16[128,512]{1,0:T(8,128)(2,1)S(1)}, u32[]{:S(2)}, u32[]{:S(2)}) collective-permute-start(bf16[128,512]{1,0:T(8,128)(2,1)S(1)} %collective-permute-done.1.refs_1_.refs_2_), channel_id=1, source_target_pairs={{0,4},{4,0},{8,12},{12,8},{1,5},{5,1},{9,13},{13,9},{2,6},{6,2},{1... | collective-permute-start | bytes 393224 | tf_op jit(solution)/shard_map/ppermute | solution.py:409
  12.2 3.4 %collective-permute-start.9 = (bf16[128,512]{1,0:T(8,128)(2,1)S(1)}, bf16[128,512]{1,0:T(8,128)(2,1)S(1)}, u32[]{:S(2)}, u32[]{:S(2)}) collective-permute-start(bf16[128,512]{1,0:T(8,128)(2,1)S(1)} %get-tuple-element.44.refs_4_), channel_id=1, source_target_pairs={{0,8},{4,12},{8,0},{12,4},{1,9},{5,13},{9,1},{13,5},{2,10},{6,14},... | collective-permute-start | bytes 393224 | tf_op jit(solution)/shard_map/ppermute | solution.py:409
  15.5 3.8 %prep.1 = (bf16[1024,4096]{1,0:T(8,128)(2,1)S(1)}, bf16[128,1024]{1,0:T(8,128)(2,1)S(1)}, bf16[128,1024]{1,0:T(8,128)(2,1)S(1)}, bf16[128,1024]{1,0:T(8,128)(2,1)S(1)}, bf16[128,1024]{1,0:T(8,128)(2,1)S(1)}) custom-call(s32[8]{0:T(128)} %order_hbm.3, bf16[1024,4096]{1,0:T(8,128)(2,1)} %w_hbm.1, bf16[256,1024]{1,0:T(8,128)(2,1)} %q_hbm.1, bf16[256,1024]{1,0:T(8,128)(2,1)} %r_hbm.1), custom_call_target="tpu_custom_call" | custom-call | flops 67108864 | bytes 16777216 | tf_op jit(solution)/shard_map/prep/pallas_call | solution.py:124
  19.3 0.0 collective-permute-done.refs_0_.refs_1_
  19.3 0.0 collective-permute-done.2.refs_2_.refs_3_
  19.3 1.4 %attend_early.1 = (bf16[128,1024]{1,0:T(8,128)(2,1)S(1)}, bf16[128,1024]{1,0:T(8,128)(2,1)S(1)}) custom-call(f32[8,128]{1,0:T(8,128)S(1)} %get-tuple-element.30.marks_ref, bf16[128,1024]{1,0:T(8,128)(2,1)S(1)} %get-tuple-element.32.q_ref, bf16[1024,4096]{1,0:T(8,128)(2,1)S(1)} %get-tuple-element.33.w_ref, ...), custom_call_target="tpu_custom_call" | custom-call | flops 536870912 | bytes 4194304 | tf_op jit(solution)/shard_map/attend_early/pallas_call | solution.py:247
  20.8 0.1 collective-permute-start.4
  20.8 0.1 collective-permute-start.8
  20.9 0.9 %collective-permute-done.9.refs_1_ = bf16[128,512]{1,0:T(8,128)(2,1)S(1)} collective-permute-done((bf16[128,512]{1,0:T(8,128)(2,1)S(1)}, bf16[128,512]{1,0:T(8,128)(2,1)S(1)}, u32[]{:S(2)}, u32[]{:S(2)}) %collective-permute-start.9) | collective-permute-done | bytes 131104 | tf_op jit(solution)/shard_map/ppermute | solution.py:409
  21.8 1.1 %collective-permute-start.10 = (bf16[128,512]{1,0:T(8,128)(2,1)S(1)}, bf16[128,512]{1,0:T(8,128)(2,1)S(1)}, u32[]{:S(2)}, u32[]{:S(2)}) collective-permute-start(bf16[128,512]{1,0:T(8,128)(2,1)S(1)} %collective-permute-done.9.refs_1_), channel_id=1, source_target_pairs={{0,4},{4,0},{8,12},{12,8},{1,5},{5,1},{9,13},{13,9},{2,6},{6,2},{1... | collective-permute-start | bytes 393224 | tf_op jit(solution)/shard_map/ppermute | solution.py:409
  22.9 1.0 %early_rest.1 = (f32[128,1024]{1,0:T(8,128)S(1)}, bf16[128,1024]{1,0:T(8,128)(2,1)S(1)}, f32[128,1024]{1,0:T(8,128)S(1)}) custom-call(bf16[128,1024]{1,0:T(8,128)(2,1)S(1)} %get-tuple-element.35.att_ref, bf16[1024,4096]{1,0:T(8,128)(2,1)S(1)} %get-tuple-element.33.w_ref), custom_call_target="tpu_custom_call" | custom-call | flops 805306368 | bytes 8388608 | tf_op jit(solution)/shard_map/early_rest/pallas_call | solution.py:304
  24.0 0.1 collective-permute-start.3
  24.0 1.5 %attend_ahead.1 = (f32[2,512,128]{2,1,0:T(8,128)S(1)}, f32[2,512,128]{2,1,0:T(8,128)S(1)}, f32[2,512,128]{2,1,0:T(8,128)S(1)}) custom-call(bf16[128,1024]{1,0:T(8,128)(2,1)S(1)} %get-tuple-element.43.q_ref, bf16[128,512]{1,0:T(8,128)(2,1)S(1)} %get-tuple-element.34.refs_3_.refs_0_, bf16[128,512]{1,0:T(8,128)(2,1)S(1)} %collective-permute-done.refs_0_.refs_1_, ...), custom_call_target="tpu_custom_call" | custom-call | flops 335544320 | bytes 4194304 | tf_op jit(solution)/shard_map/attend_ahead/pallas_call | solution.py:262
  25.6 1.7 %collective-permute-done.8.refs_0_ = bf16[128,512]{1,0:T(8,128)(2,1)S(1)} collective-permute-done((bf16[128,512]{1,0:T(8,128)(2,1)S(1)}, bf16[128,512]{1,0:T(8,128)(2,1)S(1)}, u32[]{:S(2)}, u32[]{:S(2)}) %collective-permute-start.8) | collective-permute-done | bytes 131104 | tf_op jit(solution)/shard_map/ppermute | solution.py:409
  27.3 2.3 %collective-permute-done.10.refs_2_ = bf16[128,512]{1,0:T(8,128)(2,1)S(1)} collective-permute-done((bf16[128,512]{1,0:T(8,128)(2,1)S(1)}, bf16[128,512]{1,0:T(8,128)(2,1)S(1)}, u32[]{:S(2)}, u32[]{:S(2)}) %collective-permute-start.10) | collective-permute-done | bytes 131104 | tf_op jit(solution)/shard_map/ppermute | solution.py:409
  29.5 1.3 %attend_late.1 = (bf16[128,1024]{1,0:T(8,128)(2,1)S(1)}, bf16[128,1024]{1,0:T(8,128)(2,1)S(1)}) custom-call(f32[8,128]{1,0:T(8,128)S(1)} %get-tuple-element.30.marks_ref, bf16[128,1024]{1,0:T(8,128)(2,1)S(1)} %get-tuple-element.43.q_ref, bf16[1024,4096]{1,0:T(8,128)(2,1)S(1)} %get-tuple-element.33.w_ref, f32[2,512,128]{2,1,0:T(8,128)S(1)} %get-tuple-element.45.peak_ref, ...), custom_call_target="tpu_custom_call" | custom-call | flops 469762048 | bytes 4194304 | tf_op jit(solution)/shard_map/attend_late/pallas_call | solution.py:277
  30.9 0.0 copy-start
  30.9 0.1 collective-permute-start.12
  31.0 1.0 %late_rest.1 = (f32[128,1024]{1,0:T(8,128)S(1)}, bf16[128,1024]{1,0:T(8,128)(2,1)S(1)}, f32[128,1024]{1,0:T(8,128)S(1)}) custom-call(bf16[128,1024]{1,0:T(8,128)(2,1)S(1)} %get-tuple-element.48.att_ref, bf16[1024,4096]{1,0:T(8,128)(2,1)S(1)} %get-tuple-element.33.w_ref), custom_call_target="tpu_custom_call" | custom-call | flops 805306368 | bytes 8388608 | tf_op jit(solution)/shard_map/late_rest/pallas_call | solution.py:304
  32.0 0.6 %collective-permute-start.11 = (bf16[128,1024]{1,0:T(8,128)(2,1)S(1)}, bf16[128,1024]{1,0:T(8,128)(2,1)S(1)}, u32[]{:S(2)}, u32[]{:S(2)}) collective-permute-start(bf16[128,1024]{1,0:T(8,128)(2,1)S(1)} %get-tuple-element.50), channel_id=1, source_target_pairs={{0,1},{1,0},{2,3},{3,2},{4,5},{5,4},{6,7},{7,6},{8,9},{9,8},{10,11... | collective-permute-start | bytes 786440 | tf_op jit(solution)/shard_map/ppermute | solution.py:409
  32.5 0.0 collective-permute-done.4
  32.5 0.1 add_convert_fusion.1
  32.6 1.6 %collective-permute-start.5 = (bf16[128,1024]{1,0:T(8,128)(2,1)S(1)}, bf16[128,1024]{1,0:T(8,128)(2,1)S(1)}, u32[]{:S(2)}, u32[]{:S(2)}) collective-permute-start(bf16[128,1024]{1,0:T(8,128)(2,1)S(1)} %add_convert_fusion.1), channel_id=1, source_target_pairs={{0,2},{1,3},{2,0},{3,1},{4,6},{5,7},{6,4},{7,5},{8,10},{9,11},{10,... | collective-permute-start | bytes 786440 | tf_op jit(solution)/shard_map/ppermute | solution.py:409
  34.2 0.0 collective-permute-done.12
  34.2 0.1 add_convert_fusion
  34.2 0.6 %collective-permute-start.13 = (bf16[128,1024]{1,0:T(8,128)(2,1)S(1)}, bf16[128,1024]{1,0:T(8,128)(2,1)S(1)}, u32[]{:S(2)}, u32[]{:S(2)}) collective-permute-start(bf16[128,1024]{1,0:T(8,128)(2,1)S(1)} %add_convert_fusion), channel_id=1, source_target_pairs={{0,2},{1,3},{2,0},{3,1},{4,6},{5,7},{6,4},{7,5},{8,10},{9,11},{10,... | collective-permute-start | bytes 786440 | tf_op jit(solution)/shard_map/ppermute | solution.py:409
  34.8 0.0 collective-permute-done.3.core_ref
  34.8 7.0 %collective-permute-done.5.chip_ref = bf16[128,1024]{1,0:T(8,128)(2,1)S(1)} collective-permute-done((bf16[128,1024]{1,0:T(8,128)(2,1)S(1)}, bf16[128,1024]{1,0:T(8,128)(2,1)S(1)}, u32[]{:S(2)}, u32[]{:S(2)}) %collective-permute-start.5) | collective-permute-done | bytes 262176 | tf_op jit(solution)/shard_map/ppermute | solution.py:409
  41.8 0.2 early_mix.1
  42.1 0.1 collective-permute-start.6
  42.1 0.0 collective-permute-done.11.core_ref
  42.2 4.4 %collective-permute-done.13.chip_ref = bf16[128,1024]{1,0:T(8,128)(2,1)S(1)} collective-permute-done((bf16[128,1024]{1,0:T(8,128)(2,1)S(1)}, bf16[128,1024]{1,0:T(8,128)(2,1)S(1)}, u32[]{:S(2)}, u32[]{:S(2)}) %collective-permute-start.13) | collective-permute-done | bytes 262176 | tf_op jit(solution)/shard_map/ppermute | solution.py:409
  46.5 0.2 late_mix.1
  46.7 0.1 collective-permute-start.14
  46.8 0.0 collective-permute-done.6
  46.8 1.6 %collective-permute-start.7 = (f32[8,128]{1,0:T(8,128)S(1)}, f32[8,128]{1,0:T(8,128)S(1)}, u32[]{:S(2)}, u32[]{:S(2)}) collective-permute-start(f32[8,128]{1,0:T(8,128)S(1)} %add.13.own_ref), channel_id=1, source_target_pairs={{0,2},{1,3},{2,0},{3,1},{4,6},{5,7},{6,4},{7,5},{8,10},{9,11},{10,... | collective-permute-start | bytes 12296 | tf_op jit(solution)/shard_map/ppermute | solution.py:409
  48.4 0.0 collective-permute-done.14
  48.4 1.1 %collective-permute-start.15 = (f32[8,128]{1,0:T(8,128)S(1)}, f32[8,128]{1,0:T(8,128)S(1)}, u32[]{:S(2)}, u32[]{:S(2)}) collective-permute-start(f32[8,128]{1,0:T(8,128)S(1)} %add.15.own_ref), channel_id=1, source_target_pairs={{0,2},{1,3},{2,0},{3,1},{4,6},{5,7},{6,4},{7,5},{8,10},{9,11},{10,... | collective-permute-start | bytes 12296 | tf_op jit(solution)/shard_map/ppermute | solution.py:409
  49.5 0.0 copy-done
  49.5 1.0 %collective-permute-done.7.other_ref = f32[8,128]{1,0:T(8,128)S(1)} collective-permute-done((f32[8,128]{1,0:T(8,128)S(1)}, f32[8,128]{1,0:T(8,128)S(1)}, u32[]{:S(2)}, u32[]{:S(2)}) %collective-permute-start.7) | collective-permute-done | bytes 4128 | tf_op jit(solution)/shard_map/ppermute | solution.py:409
  50.5 0.2 early_norm.1.early_ref
  50.7 1.3 %collective-permute-done.15.other_ref = f32[8,128]{1,0:T(8,128)S(1)} collective-permute-done((f32[8,128]{1,0:T(8,128)S(1)}, f32[8,128]{1,0:T(8,128)S(1)}, u32[]{:S(2)}, u32[]{:S(2)}) %collective-permute-start.15) | collective-permute-done | bytes 4128 | tf_op jit(solution)/shard_map/ppermute | solution.py:409
  52.0 1.0 %late_norm.1 = bf16[256,1024]{1,0:T(8,128)(2,1)} custom-call(f32[8,128]{1,0:T(8,128)S(1)} %get-tuple-element.30.marks_ref, bf16[1,1024]{1,0:T(2,128)(2,1)S(1)} %reshape.3.gain_ref, bf16[128,1024]{1,0:T(8,128)(2,1)S(1)} %early_norm.1.early_ref, f32[128,1024]{1,0:T(8,128)S(1)} %get-tuple-element.53.mixed_ref, f32[8,128]{1,0:T(8,128)S(1)} %add.15.own_ref, ...), custom_call_target="tpu_custom_call" | custom-call | flops 1048576 | bytes 2097152 | tf_op jit(solution)/shard_map/late_norm/pallas_call | solution.py:387
  (3 shorter events, 0.0 us)
Async XLA Ops:
  1.0 10.5 %collective-permute-start.1 = (bf16[128,512]{1,0:T(8,128)(2,1)S(1)}, bf16[128,512]{1,0:T(8,128)(2,1)S(1)}, u32[]{:S(2)}, u32[]{:S(2)}) collective-permute-start(bf16[128,512]{1,0:T(8,128)(2,1)S(1)} %get-tuple-element.34.refs_3_.refs_0_), channel_id=1, source_target_pairs={{0,8},{4,12},{8,0},{12,4},{1,9},{5,13},{9,1},{13,5},{2,10},{6,14},... | collective-permute-start | bytes 393224 | tf_op jit(solution)/shard_map/ppermute | solution.py:409
  5.1 14.2 %collective-permute-start = (bf16[128,512]{1,0:T(8,128)(2,1)S(1)}, bf16[128,512]{1,0:T(8,128)(2,1)S(1)}, u32[]{:S(2)}, u32[]{:S(2)}) collective-permute-start(bf16[128,512]{1,0:T(8,128)(2,1)S(1)} %get-tuple-element.34.refs_3_.refs_0_), channel_id=1, source_target_pairs={{0,4},{4,0},{8,12},{12,8},{1,5},{5,1},{9,13},{13,9},{2,6},{6,2},{1... | collective-permute-start | bytes 393224 | tf_op jit(solution)/shard_map/ppermute | solution.py:409
  11.5 7.8 %collective-permute-start.2 = (bf16[128,512]{1,0:T(8,128)(2,1)S(1)}, bf16[128,512]{1,0:T(8,128)(2,1)S(1)}, u32[]{:S(2)}, u32[]{:S(2)}) collective-permute-start(bf16[128,512]{1,0:T(8,128)(2,1)S(1)} %collective-permute-done.1.refs_1_.refs_2_), channel_id=1, source_target_pairs={{0,4},{4,0},{8,12},{12,8},{1,5},{5,1},{9,13},{13,9},{2,6},{6,2},{1... | collective-permute-start | bytes 393224 | tf_op jit(solution)/shard_map/ppermute | solution.py:409
  12.2 9.6 %collective-permute-start.9 = (bf16[128,512]{1,0:T(8,128)(2,1)S(1)}, bf16[128,512]{1,0:T(8,128)(2,1)S(1)}, u32[]{:S(2)}, u32[]{:S(2)}) collective-permute-start(bf16[128,512]{1,0:T(8,128)(2,1)S(1)} %get-tuple-element.44.refs_4_), channel_id=1, source_target_pairs={{0,8},{4,12},{8,0},{12,4},{1,9},{5,13},{9,1},{13,5},{2,10},{6,14},... | collective-permute-start | bytes 393224 | tf_op jit(solution)/shard_map/ppermute | solution.py:409
  20.8 11.8 %collective-permute-start.4 = (bf16[128,1024]{1,0:T(8,128)(2,1)S(1)}, bf16[128,1024]{1,0:T(8,128)(2,1)S(1)}, u32[]{:S(2)}, u32[]{:S(2)}) collective-permute-start(bf16[128,1024]{1,0:T(8,128)(2,1)S(1)} %get-tuple-element.39), channel_id=1, source_target_pairs={{0,1},{1,0},{2,3},{3,2},{4,5},{5,4},{6,7},{7,6},{8,9},{9,8},{10,11... | collective-permute-start | bytes 786440 | tf_op jit(solution)/shard_map/ppermute | solution.py:409
  20.8 6.4 %collective-permute-start.8 = (bf16[128,512]{1,0:T(8,128)(2,1)S(1)}, bf16[128,512]{1,0:T(8,128)(2,1)S(1)}, u32[]{:S(2)}, u32[]{:S(2)}) collective-permute-start(bf16[128,512]{1,0:T(8,128)(2,1)S(1)} %get-tuple-element.44.refs_4_), channel_id=1, source_target_pairs={{0,4},{4,0},{8,12},{12,8},{1,5},{5,1},{9,13},{13,9},{2,6},{6,2},{1... | collective-permute-start | bytes 393224 | tf_op jit(solution)/shard_map/ppermute | solution.py:409
  21.8 7.7 %collective-permute-start.10 = (bf16[128,512]{1,0:T(8,128)(2,1)S(1)}, bf16[128,512]{1,0:T(8,128)(2,1)S(1)}, u32[]{:S(2)}, u32[]{:S(2)}) collective-permute-start(bf16[128,512]{1,0:T(8,128)(2,1)S(1)} %collective-permute-done.9.refs_1_), channel_id=1, source_target_pairs={{0,4},{4,0},{8,12},{12,8},{1,5},{5,1},{9,13},{13,9},{2,6},{6,2},{1... | collective-permute-start | bytes 393224 | tf_op jit(solution)/shard_map/ppermute | solution.py:409
  24.0 10.9 %collective-permute-start.3 = (bf16[128,1024]{1,0:T(8,128)(2,1)S(1)}, bf16[128,1024]{1,0:T(8,128)(2,1)S(1)}, u32[]{:S(2)}, u32[]{:S(2)}) collective-permute-start(bf16[128,1024]{1,0:T(8,128)(2,1)S(1)} %get-tuple-element.37), channel_id=1, source_target_pairs={{0,1},{1,0},{2,3},{3,2},{4,5},{5,4},{6,7},{7,6},{8,9},{9,8},{10,11... | collective-permute-start | bytes 786440 | tf_op jit(solution)/shard_map/ppermute | solution.py:409
  30.9 18.6 %copy-start = (bf16[1024]{0:T(1024)(128)(2,1)S(1)}, bf16[1024]{0:T(1024)(128)(2,1)}, u32[]{:S(2)}) copy-start(bf16[1024]{0:T(1024)(128)(2,1)} %param.12) | copy-start | bytes 6148
  30.9 3.3 %collective-permute-start.12 = (bf16[128,1024]{1,0:T(8,128)(2,1)S(1)}, bf16[128,1024]{1,0:T(8,128)(2,1)S(1)}, u32[]{:S(2)}, u32[]{:S(2)}) collective-permute-start(bf16[128,1024]{1,0:T(8,128)(2,1)S(1)} %get-tuple-element.52), channel_id=1, source_target_pairs={{0,1},{1,0},{2,3},{3,2},{4,5},{5,4},{6,7},{7,6},{8,9},{9,8},{10,11... | collective-permute-start | bytes 786440 | tf_op jit(solution)/shard_map/ppermute | solution.py:409
  32.0 10.2 %collective-permute-start.11 = (bf16[128,1024]{1,0:T(8,128)(2,1)S(1)}, bf16[128,1024]{1,0:T(8,128)(2,1)S(1)}, u32[]{:S(2)}, u32[]{:S(2)}) collective-permute-start(bf16[128,1024]{1,0:T(8,128)(2,1)S(1)} %get-tuple-element.50), channel_id=1, source_target_pairs={{0,1},{1,0},{2,3},{3,2},{4,5},{5,4},{6,7},{7,6},{8,9},{9,8},{10,11... | collective-permute-start | bytes 786440 | tf_op jit(solution)/shard_map/ppermute | solution.py:409
  32.6 9.2 %collective-permute-start.5 = (bf16[128,1024]{1,0:T(8,128)(2,1)S(1)}, bf16[128,1024]{1,0:T(8,128)(2,1)S(1)}, u32[]{:S(2)}, u32[]{:S(2)}) collective-permute-start(bf16[128,1024]{1,0:T(8,128)(2,1)S(1)} %add_convert_fusion.1), channel_id=1, source_target_pairs={{0,2},{1,3},{2,0},{3,1},{4,6},{5,7},{6,4},{7,5},{8,10},{9,11},{10,... | collective-permute-start | bytes 786440 | tf_op jit(solution)/shard_map/ppermute | solution.py:409
  34.2 12.3 %collective-permute-start.13 = (bf16[128,1024]{1,0:T(8,128)(2,1)S(1)}, bf16[128,1024]{1,0:T(8,128)(2,1)S(1)}, u32[]{:S(2)}, u32[]{:S(2)}) collective-permute-start(bf16[128,1024]{1,0:T(8,128)(2,1)S(1)} %add_convert_fusion), channel_id=1, source_target_pairs={{0,2},{1,3},{2,0},{3,1},{4,6},{5,7},{6,4},{7,5},{8,10},{9,11},{10,... | collective-permute-start | bytes 786440 | tf_op jit(solution)/shard_map/ppermute | solution.py:409
  42.1 4.7 %collective-permute-start.6 = (f32[8,128]{1,0:T(8,128)S(1)}, f32[8,128]{1,0:T(8,128)S(1)}, u32[]{:S(2)}, u32[]{:S(2)}) collective-permute-start(f32[8,128]{1,0:T(8,128)S(1)} %get-tuple-element.41), channel_id=1, source_target_pairs={{0,1},{1,0},{2,3},{3,2},{4,5},{5,4},{6,7},{7,6},{8,9},{9,8},{10,11... | collective-permute-start | bytes 12296 | tf_op jit(solution)/shard_map/ppermute | solution.py:409
  46.7 1.7 %collective-permute-start.14 = (f32[8,128]{1,0:T(8,128)S(1)}, f32[8,128]{1,0:T(8,128)S(1)}, u32[]{:S(2)}, u32[]{:S(2)}) collective-permute-start(f32[8,128]{1,0:T(8,128)S(1)} %get-tuple-element.54), channel_id=1, source_target_pairs={{0,1},{1,0},{2,3},{3,2},{4,5},{5,4},{6,7},{7,6},{8,9},{9,8},{10,11... | collective-permute-start | bytes 12296 | tf_op jit(solution)/shard_map/ppermute | solution.py:409
  46.8 3.7 %collective-permute-start.7 = (f32[8,128]{1,0:T(8,128)S(1)}, f32[8,128]{1,0:T(8,128)S(1)}, u32[]{:S(2)}, u32[]{:S(2)}) collective-permute-start(f32[8,128]{1,0:T(8,128)S(1)} %add.13.own_ref), channel_id=1, source_target_pairs={{0,2},{1,3},{2,0},{3,1},{4,6},{5,7},{6,4},{7,5},{8,10},{9,11},{10,... | collective-permute-start | bytes 12296 | tf_op jit(solution)/shard_map/ppermute | solution.py:409
  48.4 3.6 %collective-permute-start.15 = (f32[8,128]{1,0:T(8,128)S(1)}, f32[8,128]{1,0:T(8,128)S(1)}, u32[]{:S(2)}, u32[]{:S(2)}) collective-permute-start(f32[8,128]{1,0:T(8,128)S(1)} %add.15.own_ref), channel_id=1, source_target_pairs={{0,2},{1,3},{2,0},{3,1},{4,6},{5,7},{6,4},{7,5},{8,10},{9,11},{10,... | collective-permute-start | bytes 12296 | tf_op jit(solution)/shard_map/ppermute | solution.py:409

commit v4 on v3

--- a/solution.py
+++ b/solution.py
@@ -149,7 +149,7 @@
         yield stacked, keys, vals
 
 
-def softmax_terms(stacked, keys, biases, diagonal):
+def masked_scores(stacked, keys, biases, diagonal):
     scores = lax.dot_general(
         stacked, keys, (((1,), (1,)), ((), ())), preferred_element_type=jnp.float32
     )
@@ -194,40 +194,30 @@
     away_ref[...] = block.astype(away_ref.dtype)
 
 
-def early_kernel(kv_heads, n_core, marks_ref, q_ref, w_ref, *refs):
-    *piece_refs, att_ref, away_ref = refs
-    rows = away_ref.shape[0]
-    biases = [marks_ref[i : i + 1, :] for i in (1, 2, 3)]
-    outs = []
-    for stacked, keys, vals in head_views(q_ref[...], [r[...] for r in piece_refs], kv_heads):
-        parts, peak = softmax_terms(stacked, keys, biases, lower(rows))
-        total, mixed = weigh(parts, peak, vals)
-        outs += unstack((mixed / total).astype(jnp.bfloat16), rows)
-    att = jnp.concatenate(outs, axis=1)
-    att_ref[...] = att
-    first_columns(att, w_ref, away_ref, n_core)
-
-
-def ahead_kernel(kv_heads, q_ref, *refs):
+def ahead_kernel(kv_heads, late, marks_ref, q_ref, *refs):
     *piece_refs, peak_ref, total_ref, mixed_ref = refs
-    rows = q_ref.shape[0]
+    rows = piece_refs[-1].shape[0]
+    biases = [None] * (len(piece_refs) - 1) if late else [marks_ref[i : i + 1, :] for i in (1, 2)]
     views = head_views(q_ref[...], [r[...] for r in piece_refs], kv_heads)
     for h, (stacked, keys, vals) in enumerate(views):
-        parts, peak = softmax_terms(stacked, keys, [None] * 4, lower(rows))
+        parts, peak = masked_scores(stacked, keys, biases, lower(rows))
         total, mixed = weigh(parts, peak, vals)
         peak_ref[h] = jnp.broadcast_to(peak, mixed.shape)
         total_ref[h] = jnp.broadcast_to(total, mixed.shape)
         mixed_ref[h] = mixed
 
 
-def late_kernel(kv_heads, n_core, marks_ref, q_ref, w_ref, peak_ref, total_ref, mixed_ref, *refs):
+def attend_kernel(
+    kv_heads, n_core, late, marks_ref, q_ref, w_ref, peak_ref, total_ref, mixed_ref, *refs
+):
     *piece_refs, att_ref, away_ref = refs
     rows = away_ref.shape[0]
-    biases = [marks_ref[i : i + 1, :] for i in (4, 5, 6)]
+    biases = [None] * (len(piece_refs) - 3) if late else []
+    biases += [marks_ref[i : i + 1, :] for i in ((4, 5, 6) if late else (3,))]
     outs = []
     views = head_views(q_ref[...], [r[...] for r in piece_refs], kv_heads)
     for h, (stacked, keys, vals) in enumerate(views):
-        parts, peak = softmax_terms(stacked, keys, biases, None)
+        parts, peak = masked_scores(stacked, keys, biases, None)
         before = peak_ref[h]
         peak = jnp.maximum(peak, before)
         factor = jnp.exp2((before - peak) * FACTOR)
@@ -240,47 +230,32 @@
     first_columns(att, w_ref, away_ref, n_core)
 
 
-def attend_early(kv_heads, n_core, marks, queries, weight, pieces):
+def attend_ahead(kv_heads, late, marks, queries, pieces):
+    rows, depth = queries.shape
+    keys = rows * len(pieces)
+    state = vmem_out((kv_heads, rows * depth // (kv_heads * HEAD_SIZE), HEAD_SIZE), jnp.float32)
+    return pl.pallas_call(
+        functools.partial(ahead_kernel, kv_heads, late),
+        out_shape=(state,) * 3,
+        in_specs=[whole(VMEM)] * (2 + len(pieces)),
+        out_specs=(whole(VMEM),) * 3,
+        compiler_params=params(),
+        name="late_ahead" if late else "early_ahead",
+        cost_estimate=cost(4 * rows * depth * keys, 4 << 20, 1 << 20),
+    )(marks, queries, *pieces)
+
+
+def attend(kv_heads, n_core, late, marks, queries, weight, state, pieces):
     rows, depth = queries.shape
     cols = weight.shape[1] // (2 * n_core)
     keys = rows * len(pieces)
     return pl.pallas_call(
-        functools.partial(early_kernel, kv_heads, n_core),
-        out_shape=(vmem_out(queries.shape, jnp.bfloat16), vmem_out((rows, cols), jnp.bfloat16)),
-        in_specs=[whole(VMEM)] * (3 + len(pieces)),
-        out_specs=(whole(VMEM),) * 2,
-        compiler_params=params(),
-        name="attend_early",
-        cost_estimate=cost(4 * rows * depth * keys + 2 * rows * depth * cols, 4 << 20, 1 << 20),
-    )(marks, queries, weight, *pieces)
-
-
-def attend_ahead(kv_heads, queries, pieces):
-    rows, depth = queries.shape
-    keys = rows * len(pieces)
-    state = vmem_out((kv_heads, rows * depth // (kv_heads * HEAD_SIZE), HEAD_SIZE), jnp.float32)
-    return pl.pallas_call(
-        functools.partial(ahead_kernel, kv_heads),
-        out_shape=(state,) * 3,
-        in_specs=[whole(VMEM)] * (1 + len(pieces)),
-        out_specs=(whole(VMEM),) * 3,
-        compiler_params=params(),
-        name="attend_ahead",
-        cost_estimate=cost(4 * rows * depth * keys, 4 << 20, 1 << 20),
-    )(queries, *pieces)
-
-
-def attend_late(kv_heads, n_core, marks, queries, weight, state, pieces):
-    rows, depth = queries.shape
-    cols = weight.shape[1] // (2 * n_core)
-    keys = rows * len(pieces)
-    return pl.pallas_call(
-        functools.partial(late_kernel, kv_heads, n_core),
+        functools.partial(attend_kernel, kv_heads, n_core, late),
         out_shape=(vmem_out(queries.shape, jnp.bfloat16), vmem_out((rows, cols), jnp.bfloat16)),
         in_specs=[whole(VMEM)] * (6 + len(pieces)),
         out_specs=(whole(VMEM),) * 2,
         compiler_params=params(),
-        name="attend_late",
+        name="attend_late" if late else "attend_early",
         cost_estimate=cost(4 * rows * depth * keys + 2 * rows * depth * cols, 4 << 20, 1 << 20),
     )(marks, queries, weight, *state, *pieces)
 
@@ -426,14 +401,15 @@
         core = send(away, "head", 1)
         return keep, core, chip
 
-    pieces = [early_a, early_b, early_c, early]
-    att, away = attend_early(kv_heads, n_core, marks, q_e, held, pieces)
+    pieces = [early_a, early_b, early]
+    state_e = attend_ahead(kv_heads, False, marks, q_e, pieces)
+    pieces = [early, early_a, early_b, late]
+    state_l = attend_ahead(kv_heads, True, marks, q_l, pieces)
+    att, away = attend(kv_heads, n_core, False, marks, q_e, held, state_e, [early_c])
     keep_e, core_e, chip_e = project(att, away, False)
 
-    pieces = [early, early_a, early_b, early_c, late]
-    state = attend_ahead(kv_heads, q_l, pieces)
-    pieces = [late_a, late_b, late_c]
-    att, away = attend_late(kv_heads, n_core, marks, q_l, held, state, pieces)
+    pieces = [early_c, late_a, late_b, late_c]
+    att, away = attend(kv_heads, n_core, True, marks, q_l, held, state_l, pieces)
     keep_l, core_l, chip_l = project(att, away, True)
 
     mixed_e, sq_e = mix(False, res_e, keep_e, core_e, chip_e)

time: 53.2 us -> 54 us (1.015)
  starting transfers between devices: 16.6 us -> 17.2 us
    ppermute x16, starting transfers between devices: 16.6 us -> 17.2 us  [send(): return lax.ppermute(x, axis, [(i, i ^ step) for i in range(size)])]
    pallas_call x3 -> x4, Pallas kernels: 4.25 us -> 4.61 us  [the longest x2 2.64 us: attend(): pl.pallas_call(functools.partial(attend_kernel, kv_heads, n_core, late),...]
  transfers between devices with their start and end apart: 16 -> 16, of which waited for: 8 -> 8; matrix products, arithmetic and copies ran while one was open for 0% -> 0% of each run, Pallas kernels for 20% -> 21%
where the time goes in v4:
time: 54 us; the launch traced here: 53.8 us
  waiting for transfers between devices  23.2 us (43%)
  starting transfers between devices  17.2 us (32%)
  Pallas kernels  13.1 us (24%)
    ppermute x16, waiting for transfers between devices, send(): return lax.ppermute(x, axis, [(i, i ^ step) for i in range(size)])  23.2 us
    ppermute x16, starting transfers between devices, send(): return lax.ppermute(x, axis, [(i, i ^ step) for i in range(size)])  17.2 us
    pallas_call x1, Pallas kernels, prep(): pl.pallas_call(prep_kernel, out_shape=(vmem_out(weight.shape, weight.dtyp...  3.75 us
    pallas_call x2, Pallas kernels, attend(): pl.pallas_call(functools.partial(attend_kernel, kv_heads, n_core, late),...  2.64 us
    pallas_call x2, Pallas kernels, project_rest(): pl.pallas_call(functools.partial(rest_kernel, n_core), out_shape=(vmem_ou...  2.02 us
    pallas_call x2, Pallas kernels, attend_ahead(): pl.pallas_call(functools.partial(ahead_kernel, kv_heads, late), out_shape...  1.97 us
  transfers between devices with their start and end apart: 16, of which 8 were waited for; matrix products, arithmetic and copies ran while one was open for 0% of the time, Pallas kernels for 21%

profile of v4, /device:TPU:0, one launch (start us, length us, event | category | flops | bytes accessed | tf_op | source)
XLA Modules:
  0.0 53.8 jit_solution(12892957424222159995)
XLA Ops:
  0.0 1.0 %split_halves.1 = (bf16[128,512]{1,0:T(8,128)(2,1)S(1)}, bf16[128,512]{1,0:T(8,128)(2,1)S(1)}, f32[8,128]{1,0:T(8,128)S(1)}) custom-call(s32[8]{0:T(128)} %order_hbm.3, bf16[256,256]{1,0:T(8,128)(2,1)} %k_hbm.1, bf16[256,256]{1,0:T(8,128)(2,1)} %v_hbm.1), custom_call_target="tpu_custom_call" | custom-call | flops 1000 | bytes 1048576 | tf_op jit(solution)/shard_map/split_halves/pallas_call | solution.py:87
  1.0 4.1 %collective-permute-start.1 = (bf16[128,512]{1,0:T(8,128)(2,1)S(1)}, bf16[128,512]{1,0:T(8,128)(2,1)S(1)}, u32[]{:S(2)}, u32[]{:S(2)}) collective-permute-start(bf16[128,512]{1,0:T(8,128)(2,1)S(1)} %get-tuple-element.37.refs_2_.refs_0_), channel_id=1, source_target_pairs={{0,8},{4,12},{8,0},{12,4},{1,9},{5,13},{9,1},{13,5},{2,10},{6,14},... | collective-permute-start | bytes 393224 | tf_op jit(solution)/shard_map/ppermute | solution.py:384
  5.1 1.6 %collective-permute-start = (bf16[128,512]{1,0:T(8,128)(2,1)S(1)}, bf16[128,512]{1,0:T(8,128)(2,1)S(1)}, u32[]{:S(2)}, u32[]{:S(2)}) collective-permute-start(bf16[128,512]{1,0:T(8,128)(2,1)S(1)} %get-tuple-element.37.refs_2_.refs_0_), channel_id=1, source_target_pairs={{0,4},{4,0},{8,12},{12,8},{1,5},{5,1},{9,13},{13,9},{2,6},{6,2},{1... | collective-permute-start | bytes 393224 | tf_op jit(solution)/shard_map/ppermute | solution.py:384
  6.7 4.8 %collective-permute-done.1.refs_1_.refs_2_ = bf16[128,512]{1,0:T(8,128)(2,1)S(1)} collective-permute-done((bf16[128,512]{1,0:T(8,128)(2,1)S(1)}, bf16[128,512]{1,0:T(8,128)(2,1)S(1)}, u32[]{:S(2)}, u32[]{:S(2)}) %collective-permute-start.1) | collective-permute-done | bytes 131104 | tf_op jit(solution)/shard_map/ppermute | solution.py:384
  11.5 0.6 %collective-permute-start.2 = (bf16[128,512]{1,0:T(8,128)(2,1)S(1)}, bf16[128,512]{1,0:T(8,128)(2,1)S(1)}, u32[]{:S(2)}, u32[]{:S(2)}) collective-permute-start(bf16[128,512]{1,0:T(8,128)(2,1)S(1)} %collective-permute-done.1.refs_1_.refs_2_), channel_id=1, source_target_pairs={{0,4},{4,0},{8,12},{12,8},{1,5},{5,1},{9,13},{13,9},{2,6},{6,2},{1... | collective-permute-start | bytes 393224 | tf_op jit(solution)/shard_map/ppermute | solution.py:384
  12.2 3.4 %collective-permute-start.9 = (bf16[128,512]{1,0:T(8,128)(2,1)S(1)}, bf16[128,512]{1,0:T(8,128)(2,1)S(1)}, u32[]{:S(2)}, u32[]{:S(2)}) collective-permute-start(bf16[128,512]{1,0:T(8,128)(2,1)S(1)} %get-tuple-element.50.refs_3_), channel_id=1, source_target_pairs={{0,8},{4,12},{8,0},{12,4},{1,9},{5,13},{9,1},{13,5},{2,10},{6,14},... | collective-permute-start | bytes 393224 | tf_op jit(solution)/shard_map/ppermute | solution.py:384
  15.5 3.8 %prep.1 = (bf16[1024,4096]{1,0:T(8,128)(2,1)S(1)}, bf16[128,1024]{1,0:T(8,128)(2,1)S(1)}, bf16[128,1024]{1,0:T(8,128)(2,1)S(1)}, bf16[128,1024]{1,0:T(8,128)(2,1)S(1)}, bf16[128,1024]{1,0:T(8,128)(2,1)S(1)}) custom-call(s32[8]{0:T(128)} %order_hbm.3, bf16[1024,4096]{1,0:T(8,128)(2,1)} %w_hbm.1, bf16[256,1024]{1,0:T(8,128)(2,1)} %q_hbm.1, bf16[256,1024]{1,0:T(8,128)(2,1)} %r_hbm.1), custom_call_target="tpu_custom_call" | custom-call | flops 67108864 | bytes 16777216 | tf_op jit(solution)/shard_map/prep/pallas_call | solution.py:124
  19.3 0.0 collective-permute-done.refs_0_.refs_1_
  19.3 0.9 %early_ahead.1 = (f32[2,512,128]{2,1,0:T(8,128)S(1)}, f32[2,512,128]{2,1,0:T(8,128)S(1)}, f32[2,512,128]{2,1,0:T(8,128)S(1)}) custom-call(f32[8,128]{1,0:T(8,128)S(1)} %get-tuple-element.33.marks_ref, bf16[128,1024]{1,0:T(8,128)(2,1)S(1)} %get-tuple-element.35.q_ref, bf16[128,512]{1,0:T(8,128)(2,1)S(1)} %collective-permute-done.refs_0_.refs_1_, ...), custom_call_target="tpu_custom_call" | custom-call | flops 201326592 | bytes 4194304 | tf_op jit(solution)/shard_map/early_ahead/pallas_call | solution.py:237
  20.2 0.0 collective-permute-done.2.refs_0_
  20.2 1.1 %attend_early.1 = (bf16[128,1024]{1,0:T(8,128)(2,1)S(1)}, bf16[128,1024]{1,0:T(8,128)(2,1)S(1)}) custom-call(f32[8,128]{1,0:T(8,128)S(1)} %get-tuple-element.33.marks_ref, bf16[128,1024]{1,0:T(8,128)(2,1)S(1)} %get-tuple-element.35.q_ref, bf16[1024,4096]{1,0:T(8,128)(2,1)S(1)} %get-tuple-element.36.w_ref, f32[2,512,128]{2,1,0:T(8,128)S(1)} %get-tuple-element.38.peak_ref, ...), custom_call_target="tpu_custom_call" | custom-call | flops 335544320 | bytes 4194304 | tf_op jit(solution)/shard_map/attend_early/pallas_call | solution.py:252
  21.4 0.1 collective-permute-start.4
  21.4 0.1 collective-permute-start.8
  21.5 0.3 collective-permute-done.9.refs_2_
  21.8 1.7 %collective-permute-start.10 = (bf16[128,512]{1,0:T(8,128)(2,1)S(1)}, bf16[128,512]{1,0:T(8,128)(2,1)S(1)}, u32[]{:S(2)}, u32[]{:S(2)}) collective-permute-start(bf16[128,512]{1,0:T(8,128)(2,1)S(1)} %collective-permute-done.9.refs_2_), channel_id=1, source_target_pairs={{0,4},{4,0},{8,12},{12,8},{1,5},{5,1},{9,13},{13,9},{2,6},{6,2},{1... | collective-permute-start | bytes 393224 | tf_op jit(solution)/shard_map/ppermute | solution.py:384
  23.5 1.1 %late_ahead.1 = (f32[2,512,128]{2,1,0:T(8,128)S(1)}, f32[2,512,128]{2,1,0:T(8,128)S(1)}, f32[2,512,128]{2,1,0:T(8,128)S(1)}) custom-call(f32[8,128]{1,0:T(8,128)S(1)} %get-tuple-element.33.marks_ref, bf16[128,1024]{1,0:T(8,128)(2,1)S(1)} %get-tuple-element.49.q_ref, bf16[128,512]{1,0:T(8,128)(2,1)S(1)} %get-tuple-element.37.refs_2_.refs_0_, ...), custom_call_target="tpu_custom_call" | custom-call | flops 268435456 | bytes 4194304 | tf_op jit(solution)/shard_map/late_ahead/pallas_call | solution.py:237
  24.6 1.0 %early_rest.1 = (f32[128,1024]{1,0:T(8,128)S(1)}, bf16[128,1024]{1,0:T(8,128)(2,1)S(1)}, f32[128,1024]{1,0:T(8,128)S(1)}) custom-call(bf16[128,1024]{1,0:T(8,128)(2,1)S(1)} %get-tuple-element.41.att_ref, bf16[1024,4096]{1,0:T(8,128)(2,1)S(1)} %get-tuple-element.36.w_ref), custom_call_target="tpu_custom_call" | custom-call | flops 805306368 | bytes 8388608 | tf_op jit(solution)/shard_map/early_rest/pallas_call | solution.py:279
  25.6 0.1 collective-permute-start.3
  25.7 2.2 %collective-permute-done.8.refs_1_ = bf16[128,512]{1,0:T(8,128)(2,1)S(1)} collective-permute-done((bf16[128,512]{1,0:T(8,128)(2,1)S(1)}, bf16[128,512]{1,0:T(8,128)(2,1)S(1)}, u32[]{:S(2)}, u32[]{:S(2)}) %collective-permute-start.8) | collective-permute-done | bytes 131104 | tf_op jit(solution)/shard_map/ppermute | solution.py:384
  27.9 2.3 %collective-permute-done.10.refs_3_ = bf16[128,512]{1,0:T(8,128)(2,1)S(1)} collective-permute-done((bf16[128,512]{1,0:T(8,128)(2,1)S(1)}, bf16[128,512]{1,0:T(8,128)(2,1)S(1)}, u32[]{:S(2)}, u32[]{:S(2)}) %collective-permute-start.10) | collective-permute-done | bytes 131104 | tf_op jit(solution)/shard_map/ppermute | solution.py:384
  30.1 1.5 %attend_late.1 = (bf16[128,1024]{1,0:T(8,128)(2,1)S(1)}, bf16[128,1024]{1,0:T(8,128)(2,1)S(1)}) custom-call(f32[8,128]{1,0:T(8,128)S(1)} %get-tuple-element.33.marks_ref, bf16[128,1024]{1,0:T(8,128)(2,1)S(1)} %get-tuple-element.49.q_ref, bf16[1024,4096]{1,0:T(8,128)(2,1)S(1)} %get-tuple-element.36.w_ref, f32[2,512,128]{2,1,0:T(8,128)S(1)} %get-tuple-element.51.peak_ref, ...), custom_call_target="tpu_custom_call" | custom-call | flops 536870912 | bytes 4194304 | tf_op jit(solution)/shard_map/attend_late/pallas_call | solution.py:252
  31.7 0.0 copy-start
  31.7 0.1 collective-permute-start.12
  31.8 1.0 %late_rest.1 = (f32[128,1024]{1,0:T(8,128)S(1)}, bf16[128,1024]{1,0:T(8,128)(2,1)S(1)}, f32[128,1024]{1,0:T(8,128)S(1)}) custom-call(bf16[128,1024]{1,0:T(8,128)(2,1)S(1)} %get-tuple-element.54.att_ref, bf16[1024,4096]{1,0:T(8,128)(2,1)S(1)} %get-tuple-element.36.w_ref), custom_call_target="tpu_custom_call" | custom-call | flops 805306368 | bytes 8388608 | tf_op jit(solution)/shard_map/late_rest/pallas_call | solution.py:279
  32.8 0.5 %collective-permute-start.11 = (bf16[128,1024]{1,0:T(8,128)(2,1)S(1)}, bf16[128,1024]{1,0:T(8,128)(2,1)S(1)}, u32[]{:S(2)}, u32[]{:S(2)}) collective-permute-start(bf16[128,1024]{1,0:T(8,128)(2,1)S(1)} %get-tuple-element.56), channel_id=1, source_target_pairs={{0,1},{1,0},{2,3},{3,2},{4,5},{5,4},{6,7},{7,6},{8,9},{9,8},{10,11... | collective-permute-start | bytes 786440 | tf_op jit(solution)/shard_map/ppermute | solution.py:384
  33.3 0.0 collective-permute-done.4
  33.3 0.1 add_convert_fusion.1
  33.4 1.6 %collective-permute-start.5 = (bf16[128,1024]{1,0:T(8,128)(2,1)S(1)}, bf16[128,1024]{1,0:T(8,128)(2,1)S(1)}, u32[]{:S(2)}, u32[]{:S(2)}) collective-permute-start(bf16[128,1024]{1,0:T(8,128)(2,1)S(1)} %add_convert_fusion.1), channel_id=1, source_target_pairs={{0,2},{1,3},{2,0},{3,1},{4,6},{5,7},{6,4},{7,5},{8,10},{9,11},{10,... | collective-permute-start | bytes 786440 | tf_op jit(solution)/shard_map/ppermute | solution.py:384
  35.0 0.0 collective-permute-done.12
  35.0 0.1 add_convert_fusion
  35.0 0.6 %collective-permute-start.13 = (bf16[128,1024]{1,0:T(8,128)(2,1)S(1)}, bf16[128,1024]{1,0:T(8,128)(2,1)S(1)}, u32[]{:S(2)}, u32[]{:S(2)}) collective-permute-start(bf16[128,1024]{1,0:T(8,128)(2,1)S(1)} %add_convert_fusion), channel_id=1, source_target_pairs={{0,2},{1,3},{2,0},{3,1},{4,6},{5,7},{6,4},{7,5},{8,10},{9,11},{10,... | collective-permute-start | bytes 786440 | tf_op jit(solution)/shard_map/ppermute | solution.py:384
  35.6 0.0 collective-permute-done.3.core_ref
  35.6 7.0 %collective-permute-done.5.chip_ref = bf16[128,1024]{1,0:T(8,128)(2,1)S(1)} collective-permute-done((bf16[128,1024]{1,0:T(8,128)(2,1)S(1)}, bf16[128,1024]{1,0:T(8,128)(2,1)S(1)}, u32[]{:S(2)}, u32[]{:S(2)}) %collective-permute-start.5) | collective-permute-done | bytes 262176 | tf_op jit(solution)/shard_map/ppermute | solution.py:384
  42.6 0.2 early_mix.1
  42.9 0.1 collective-permute-start.6
  43.0 0.0 collective-permute-done.11.core_ref
  43.0 4.4 %collective-permute-done.13.chip_ref = bf16[128,1024]{1,0:T(8,128)(2,1)S(1)} collective-permute-done((bf16[128,1024]{1,0:T(8,128)(2,1)S(1)}, bf16[128,1024]{1,0:T(8,128)(2,1)S(1)}, u32[]{:S(2)}, u32[]{:S(2)}) %collective-permute-start.13) | collective-permute-done | bytes 262176 | tf_op jit(solution)/shard_map/ppermute | solution.py:384
  47.3 0.2 late_mix.1
  47.5 0.1 collective-permute-start.14
  47.6 0.0 collective-permute-done.6
  47.6 1.6 %collective-permute-start.7 = (f32[8,128]{1,0:T(8,128)S(1)}, f32[8,128]{1,0:T(8,128)S(1)}, u32[]{:S(2)}, u32[]{:S(2)}) collective-permute-start(f32[8,128]{1,0:T(8,128)S(1)} %add.13.own_ref), channel_id=1, source_target_pairs={{0,2},{1,3},{2,0},{3,1},{4,6},{5,7},{6,4},{7,5},{8,10},{9,11},{10,... | collective-permute-start | bytes 12296 | tf_op jit(solution)/shard_map/ppermute | solution.py:384
  49.2 0.0 collective-permute-done.14
  49.2 1.1 %collective-permute-start.15 = (f32[8,128]{1,0:T(8,128)S(1)}, f32[8,128]{1,0:T(8,128)S(1)}, u32[]{:S(2)}, u32[]{:S(2)}) collective-permute-start(f32[8,128]{1,0:T(8,128)S(1)} %add.15.own_ref), channel_id=1, source_target_pairs={{0,2},{1,3},{2,0},{3,1},{4,6},{5,7},{6,4},{7,5},{8,10},{9,11},{10,... | collective-permute-start | bytes 12296 | tf_op jit(solution)/shard_map/ppermute | solution.py:384
  50.3 0.0 copy-done
  50.3 1.0 %collective-permute-done.7.other_ref = f32[8,128]{1,0:T(8,128)S(1)} collective-permute-done((f32[8,128]{1,0:T(8,128)S(1)}, f32[8,128]{1,0:T(8,128)S(1)}, u32[]{:S(2)}, u32[]{:S(2)}) %collective-permute-start.7) | collective-permute-done | bytes 4128 | tf_op jit(solution)/shard_map/ppermute | solution.py:384
  51.3 0.2 early_norm.1.early_ref
  51.5 1.3 %collective-permute-done.15.other_ref = f32[8,128]{1,0:T(8,128)S(1)} collective-permute-done((f32[8,128]{1,0:T(8,128)S(1)}, f32[8,128]{1,0:T(8,128)S(1)}, u32[]{:S(2)}, u32[]{:S(2)}) %collective-permute-start.15) | collective-permute-done | bytes 4128 | tf_op jit(solution)/shard_map/ppermute | solution.py:384
  52.8 1.0 %late_norm.1 = bf16[256,1024]{1,0:T(8,128)(2,1)} custom-call(f32[8,128]{1,0:T(8,128)S(1)} %get-tuple-element.33.marks_ref, bf16[1,1024]{1,0:T(2,128)(2,1)S(1)} %reshape.3.gain_ref, bf16[128,1024]{1,0:T(8,128)(2,1)S(1)} %early_norm.1.early_ref, f32[128,1024]{1,0:T(8,128)S(1)} %get-tuple-element.59.mixed_ref, f32[8,128]{1,0:T(8,128)S(1)} %add.15.own_ref, ...), custom_call_target="tpu_custom_call" | custom-call | flops 1048576 | bytes 2097152 | tf_op jit(solution)/shard_map/late_norm/pallas_call | solution.py:362
  (3 shorter events, 0.0 us)
Async XLA Ops:
  1.0 10.5 %collective-permute-start.1 = (bf16[128,512]{1,0:T(8,128)(2,1)S(1)}, bf16[128,512]{1,0:T(8,128)(2,1)S(1)}, u32[]{:S(2)}, u32[]{:S(2)}) collective-permute-start(bf16[128,512]{1,0:T(8,128)(2,1)S(1)} %get-tuple-element.37.refs_2_.refs_0_), channel_id=1, source_target_pairs={{0,8},{4,12},{8,0},{12,4},{1,9},{5,13},{9,1},{13,5},{2,10},{6,14},... | collective-permute-start | bytes 393224 | tf_op jit(solution)/shard_map/ppermute | solution.py:384
  5.1 14.2 %collective-permute-start = (bf16[128,512]{1,0:T(8,128)(2,1)S(1)}, bf16[128,512]{1,0:T(8,128)(2,1)S(1)}, u32[]{:S(2)}, u32[]{:S(2)}) collective-permute-start(bf16[128,512]{1,0:T(8,128)(2,1)S(1)} %get-tuple-element.37.refs_2_.refs_0_), channel_id=1, source_target_pairs={{0,4},{4,0},{8,12},{12,8},{1,5},{5,1},{9,13},{13,9},{2,6},{6,2},{1... | collective-permute-start | bytes 393224 | tf_op jit(solution)/shard_map/ppermute | solution.py:384
  11.5 8.7 %collective-permute-start.2 = (bf16[128,512]{1,0:T(8,128)(2,1)S(1)}, bf16[128,512]{1,0:T(8,128)(2,1)S(1)}, u32[]{:S(2)}, u32[]{:S(2)}) collective-permute-start(bf16[128,512]{1,0:T(8,128)(2,1)S(1)} %collective-permute-done.1.refs_1_.refs_2_), channel_id=1, source_target_pairs={{0,4},{4,0},{8,12},{12,8},{1,5},{5,1},{9,13},{13,9},{2,6},{6,2},{1... | collective-permute-start | bytes 393224 | tf_op jit(solution)/shard_map/ppermute | solution.py:384
  12.2 9.6 %collective-permute-start.9 = (bf16[128,512]{1,0:T(8,128)(2,1)S(1)}, bf16[128,512]{1,0:T(8,128)(2,1)S(1)}, u32[]{:S(2)}, u32[]{:S(2)}) collective-permute-start(bf16[128,512]{1,0:T(8,128)(2,1)S(1)} %get-tuple-element.50.refs_3_), channel_id=1, source_target_pairs={{0,8},{4,12},{8,0},{12,4},{1,9},{5,13},{9,1},{13,5},{2,10},{6,14},... | collective-permute-start | bytes 393224 | tf_op jit(solution)/shard_map/ppermute | solution.py:384
  21.4 12.0 %collective-permute-start.4 = (bf16[128,1024]{1,0:T(8,128)(2,1)S(1)}, bf16[128,1024]{1,0:T(8,128)(2,1)S(1)}, u32[]{:S(2)}, u32[]{:S(2)}) collective-permute-start(bf16[128,1024]{1,0:T(8,128)(2,1)S(1)} %get-tuple-element.45), channel_id=1, source_target_pairs={{0,1},{1,0},{2,3},{3,2},{4,5},{5,4},{6,7},{7,6},{8,9},{9,8},{10,11... | collective-permute-start | bytes 786440 | tf_op jit(solution)/shard_map/ppermute | solution.py:384
  21.4 6.4 %collective-permute-start.8 = (bf16[128,512]{1,0:T(8,128)(2,1)S(1)}, bf16[128,512]{1,0:T(8,128)(2,1)S(1)}, u32[]{:S(2)}, u32[]{:S(2)}) collective-permute-start(bf16[128,512]{1,0:T(8,128)(2,1)S(1)} %get-tuple-element.50.refs_3_), channel_id=1, source_target_pairs={{0,4},{4,0},{8,12},{12,8},{1,5},{5,1},{9,13},{13,9},{2,6},{6,2},{1... | collective-permute-start | bytes 393224 | tf_op jit(solution)/shard_map/ppermute | solution.py:384
  21.8 8.3 %collective-permute-start.10 = (bf16[128,512]{1,0:T(8,128)(2,1)S(1)}, bf16[128,512]{1,0:T(8,128)(2,1)S(1)}, u32[]{:S(2)}, u32[]{:S(2)}) collective-permute-start(bf16[128,512]{1,0:T(8,128)(2,1)S(1)} %collective-permute-done.9.refs_2_), channel_id=1, source_target_pairs={{0,4},{4,0},{8,12},{12,8},{1,5},{5,1},{9,13},{13,9},{2,6},{6,2},{1... | collective-permute-start | bytes 393224 | tf_op jit(solution)/shard_map/ppermute | solution.py:384
  25.6 10.0 %collective-permute-start.3 = (bf16[128,1024]{1,0:T(8,128)(2,1)S(1)}, bf16[128,1024]{1,0:T(8,128)(2,1)S(1)}, u32[]{:S(2)}, u32[]{:S(2)}) collective-permute-start(bf16[128,1024]{1,0:T(8,128)(2,1)S(1)} %get-tuple-element.43), channel_id=1, source_target_pairs={{0,1},{1,0},{2,3},{3,2},{4,5},{5,4},{6,7},{7,6},{8,9},{9,8},{10,11... | collective-permute-start | bytes 786440 | tf_op jit(solution)/shard_map/ppermute | solution.py:384
  31.7 18.6 %copy-start = (bf16[1024]{0:T(1024)(128)(2,1)S(1)}, bf16[1024]{0:T(1024)(128)(2,1)}, u32[]{:S(2)}) copy-start(bf16[1024]{0:T(1024)(128)(2,1)} %param.12) | copy-start | bytes 6148
  31.7 3.3 %collective-permute-start.12 = (bf16[128,1024]{1,0:T(8,128)(2,1)S(1)}, bf16[128,1024]{1,0:T(8,128)(2,1)S(1)}, u32[]{:S(2)}, u32[]{:S(2)}) collective-permute-start(bf16[128,1024]{1,0:T(8,128)(2,1)S(1)} %get-tuple-element.58), channel_id=1, source_target_pairs={{0,1},{1,0},{2,3},{3,2},{4,5},{5,4},{6,7},{7,6},{8,9},{9,8},{10,11... | collective-permute-start | bytes 786440 | tf_op jit(solution)/shard_map/ppermute | solution.py:384
  32.8 10.2 %collective-permute-start.11 = (bf16[128,1024]{1,0:T(8,128)(2,1)S(1)}, bf16[128,1024]{1,0:T(8,128)(2,1)S(1)}, u32[]{:S(2)}, u32[]{:S(2)}) collective-permute-start(bf16[128,1024]{1,0:T(8,128)(2,1)S(1)} %get-tuple-element.56), channel_id=1, source_target_pairs={{0,1},{1,0},{2,3},{3,2},{4,5},{5,4},{6,7},{7,6},{8,9},{9,8},{10,11... | collective-permute-start | bytes 786440 | tf_op jit(solution)/shard_map/ppermute | solution.py:384
  33.4 9.2 %collective-permute-start.5 = (bf16[128,1024]{1,0:T(8,128)(2,1)S(1)}, bf16[128,1024]{1,0:T(8,128)(2,1)S(1)}, u32[]{:S(2)}, u32[]{:S(2)}) collective-permute-start(bf16[128,1024]{1,0:T(8,128)(2,1)S(1)} %add_convert_fusion.1), channel_id=1, source_target_pairs={{0,2},{1,3},{2,0},{3,1},{4,6},{5,7},{6,4},{7,5},{8,10},{9,11},{10,... | collective-permute-start | bytes 786440 | tf_op jit(solution)/shard_map/ppermute | solution.py:384
  35.0 12.3 %collective-permute-start.13 = (bf16[128,1024]{1,0:T(8,128)(2,1)S(1)}, bf16[128,1024]{1,0:T(8,128)(2,1)S(1)}, u32[]{:S(2)}, u32[]{:S(2)}) collective-permute-start(bf16[128,1024]{1,0:T(8,128)(2,1)S(1)} %add_convert_fusion), channel_id=1, source_target_pairs={{0,2},{1,3},{2,0},{3,1},{4,6},{5,7},{6,4},{7,5},{8,10},{9,11},{10,... | collective-permute-start | bytes 786440 | tf_op jit(solution)/shard_map/ppermute | solution.py:384
  42.9 4.7 %collective-permute-start.6 = (f32[8,128]{1,0:T(8,128)S(1)}, f32[8,128]{1,0:T(8,128)S(1)}, u32[]{:S(2)}, u32[]{:S(2)}) collective-permute-start(f32[8,128]{1,0:T(8,128)S(1)} %get-tuple-element.47), channel_id=1, source_target_pairs={{0,1},{1,0},{2,3},{3,2},{4,5},{5,4},{6,7},{7,6},{8,9},{9,8},{10,11... | collective-permute-start | bytes 12296 | tf_op jit(solution)/shard_map/ppermute | solution.py:384
  47.5 1.7 %collective-permute-start.14 = (f32[8,128]{1,0:T(8,128)S(1)}, f32[8,128]{1,0:T(8,128)S(1)}, u32[]{:S(2)}, u32[]{:S(2)}) collective-permute-start(f32[8,128]{1,0:T(8,128)S(1)} %get-tuple-element.60), channel_id=1, source_target_pairs={{0,1},{1,0},{2,3},{3,2},{4,5},{5,4},{6,7},{7,6},{8,9},{9,8},{10,11... | collective-permute-start | bytes 12296 | tf_op jit(solution)/shard_map/ppermute | solution.py:384
  47.6 3.7 %collective-permute-start.7 = (f32[8,128]{1,0:T(8,128)S(1)}, f32[8,128]{1,0:T(8,128)S(1)}, u32[]{:S(2)}, u32[]{:S(2)}) collective-permute-start(f32[8,128]{1,0:T(8,128)S(1)} %add.13.own_ref), channel_id=1, source_target_pairs={{0,2},{1,3},{2,0},{3,1},{4,6},{5,7},{6,4},{7,5},{8,10},{9,11},{10,... | collective-permute-start | bytes 12296 | tf_op jit(solution)/shard_map/ppermute | solution.py:384
  49.2 3.6 %collective-permute-start.15 = (f32[8,128]{1,0:T(8,128)S(1)}, f32[8,128]{1,0:T(8,128)S(1)}, u32[]{:S(2)}, u32[]{:S(2)}) collective-permute-start(f32[8,128]{1,0:T(8,128)S(1)} %add.15.own_ref), channel_id=1, source_target_pairs={{0,2},{1,3},{2,0},{3,1},{4,6},{5,7},{6,4},{7,5},{8,10},{9,11},{10,... | collective-permute-start | bytes 12296 | tf_op jit(solution)/shard_map/ppermute | solution.py:384
